TPU v7x, 128 devices: a whole 4x4x4 slice. The times are simulated.
128 devices in a mesh: rep: 1, dp: 128 (over x, y, z, core).
Axes of the slice: x: 4, y: 4, z: 4, core: 2. Of those that a mesh axis runs over, the one named last changes fastest.
Arguments:
- x: bfloat16 [128, 1024, 1024], P(('rep', 'dp'))
- dy: bfloat16 [128, 1024, 1024], P(('rep', 'dp'))
- w_gate: bfloat16 [2, 1024, 3328], replicated
- w_up: bfloat16 [2, 1024, 3328], replicated
- w_down: bfloat16 [2, 3328, 1024], replicated
- m_w_gate: float32 [2, 1024, 3328], replicated
- m_w_up: float32 [2, 1024, 3328], replicated
- m_w_down: float32 [2, 3328, 1024], replicated
- v_w_gate: float32 [2, 1024, 3328], replicated
- v_w_up: float32 [2, 1024, 3328], replicated
- v_w_down: float32 [2, 3328, 1024], replicated
Outputs:
- output 1: bfloat16 [2, 1024, 3328], P('rep')
- output 2: bfloat16 [2, 1024, 3328], P('rep')
- output 3: bfloat16 [2, 3328, 1024], P('rep')
- output 4: float32 [2, 1024, 3328], P('rep')
- output 5: float32 [2, 1024, 3328], P('rep')
- output 6: float32 [2, 3328, 1024], P('rep')
- output 7: float32 [2, 1024, 3328], P('rep')
- output 8: float32 [2, 1024, 3328], P('rep')
- output 9: float32 [2, 3328, 1024], P('rep')
All inputs are finite; a program needn't handle non-finite values.
Results may differ from a plain program's by a relative error of at most 0.022.
Values are sent between devices in bfloat16 or wider.
A program may use at most 1.5 GiB of HBM per device.

v0:
```python
import jax
import jax.numpy as jnp
from jax import lax
from jax.sharding import PartitionSpec as P

NAMES = ("w_gate", "w_up", "w_down")


def matmul(a, w):
    return jnp.dot(a, w, preferred_element_type=jnp.float32).astype(jnp.bfloat16)


def normed(h):
    wide = h.astype(jnp.float32)
    scale = lax.rsqrt(jnp.mean(wide**2, -1, keepdims=True) + 1e-6)
    return (wide * scale).astype(jnp.bfloat16)


def layer(h, w):
    a = normed(h)
    gate = jnp.dot(a, w["w_gate"], preferred_element_type=jnp.float32)
    up = jnp.dot(a, w["w_up"], preferred_element_type=jnp.float32)
    return h + matmul((jax.nn.silu(gate) * up).astype(jnp.bfloat16), w["w_down"])


def adamw(w, m, v, g):
    m = 0.9 * m + 0.1 * g
    v = 0.95 * v + 0.05 * g * g
    step = m * lax.rsqrt(v + 1e-8) + 0.1 * w
    return (w - 0.02 * step).astype(jnp.bfloat16), m, v


def solution(mesh):
    def step(x, dy, *arrays):
        weights, m, v = (arrays[i : i + 3] for i in (0, 3, 6))
        layers = weights[0].shape[0]
        h, kept = x[0], []
        for number in range(layers):
            kept.append(h)
            h = layer(h, {name: w[number] for name, w in zip(NAMES, weights, strict=True)})
        by_h, summed = dy[0], [None] * layers
        for number in reversed(range(layers)):
            _, back = jax.vjp(lambda w, h: layer(h, w), {name: w[number] for name, w in zip(NAMES, weights, strict=True)}, kept[number])
            by_w, by_h = back(by_h)
            summed[number] = [lax.psum(by_w[name], "dp") for name in NAMES]
        gradients = [jnp.stack([summed[number][i] for number in range(layers)]).astype(jnp.float32) for i in range(3)]
        new = [adamw(w.astype(jnp.float32), m, v, g) for w, m, v, g in zip(weights, m, v, gradients, strict=True)]
        return tuple(one[which] for which in range(3) for one in new)

    return jax.shard_map(
        step,
        mesh=mesh,
        in_specs=(P(("rep", "dp"), None, None),) * 2 + (P(None, None, None),) * 9,
        out_specs=(P("rep", None, None),) * 9,
        check_vma=False,
    )
```

profile of v0, /device:TPU:0, one launch (start us, length us, event | category | flops | bytes accessed | tf_op | source)
XLA Modules:
  0.0 683.4 jit_solution(12610355897651021390)
XLA Ops:
  7.2 0.0 all-reduce.3.cloned.1.call-start
  7.2 2.9 copy.20
  10.1 0.0 copy-start.1
  10.1 0.5 fusion.66
  10.6 0.0 slice-start.4
  10.6 4.2 copy.21
  14.8 12.6 %convolution_convert_fusion.4 = bf16[1024,3328]{1,0:T(8,128)(2,1)} fusion(bf16[2,3328,1024]{2,1,0:T(8,128)(2,1)} %param.15, bf16[1,1024,1024]{2,1,0:T(8,128)(2,1)} %param.12), kind=kOutput, calls=%fused_computation.59 | convolution fusion | flops 6982729728 | bytes 15728640 | tf_op jit(solution)/shard_map/transpose(jvp())/dot_general | solution.py:10
  27.4 0.0 slice-done.4
  27.4 0.0 slice-done.5
  27.4 0.0 slice-done.6
  27.5 0.0 slice-done.7
  27.5 0.0 copy-done.6
  27.5 10.1 %fusion.46 = f32[1024,3328]{1,0:T(8,128)} fusion(bf16[2,1024,3328]{2,1,0:T(8,128)(2,1)S(1)} %bitcast.77, bf16[1,1024,1024]{2,1,0:T(8,128)(2,1)S(1)} %copy-done.6, f32[1024]{0:T(1024)S(1)} %add_rsqrt_fusion), kind=kOutput, calls=%fused_computation.77 | convolution fusion | flops 6982467584 | bytes 22548480 | tf_op jit(solution)/shard_map/dot_general | solution.py:21
  37.6 0.0 copy-done.10
  37.6 17.0 %multiply_convert_fusion.1 = (bf16[1024,3328]{1,0:T(8,128)(2,1)}, f32[1024,3328]{1,0:T(8,128)}) fusion(f32[1024,3328]{1,0:T(8,128)} %fusion.46, bf16[2,1024,3328]{2,1,0:T(8,128)(2,1)} %param.14, bf16[1,1024,1024]{2,1,0:T(8,128)(2,1)} %param.11, f32[1024]{0:T(1024)S(1)} %add_rsqrt_fusion), kind=kOutput, calls=%fused_computation.47 | convolution fusion | flops 7002914816 | bytes 42995712 | tf_op jit(solution)/shard_map/dot_general | solution.py:22
  54.6 0.0 copy-done.1
  54.6 11.9 %fusion.70 = (f32[1024]{0:T(1024)S(1)}, bf16[1024,1024]{0,1:T(8,128)(2,1)S(1)}) fusion(bf16[1024,3328]{1,0:T(8,128)(2,1)} %get-tuple-element.24, bf16[2,3328,1024]{2,1,0:T(8,128)(2,1)} %param.15, bf16[1,1024,1024]{1,2,0:T(8,128)(2,1)S(1)} %copy.20), kind=kOutput, calls=%fused_computation.102 | convolution fusion | flops 6984563712 | bytes 17829888 | tf_op jit(solution)/shard_map/dot_general | solution.py:10
  66.5 0.0 copy-start.3
  66.5 0.0 copy-start.8
  66.6 1.3 copy-done.3
  67.8 13.4 %fusion.33 = f32[1024,3328]{1,0:T(8,128)} fusion(bf16[2,1024,3328]{2,1,0:T(8,128)(2,1)} %param.14, bf16[1024,1024]{0,1:T(8,128)(2,1)S(1)} %get-tuple-element.27, f32[1024]{0:T(1024)S(1)} %fusion.90), kind=kOutput, calls=%fused_computation.64 | convolution fusion | flops 6982467584 | bytes 22548480 | tf_op jit(solution)/shard_map/jvp()/dot_general | solution.py:22
  81.2 24.0 %fusion.17 = (bf16[1024,3328]{1,0:T(8,128)(2,1)}, f32[1024,3328]{1,0:T(8,128)}) fusion(f32[1024,3328]{1,0:T(8,128)} %fusion.33, bf16[1024,3328]{1,0:T(8,128)(2,1)} %convolution_convert_fusion.4, bf16[2,1024,3328]{2,1,0:T(8,128)(2,1)} %param.13, bf16[1024,1024]{0,1:T(8,128)(2,1)} %copy-done.3, f32[1024]{0:T(1024)S(1)} %fusion.90), kind=kOutput, calls=%fused_computation.35 | convolution fusion | flops 7023362048 | bytes 49811456 | tf_op jit(solution)/shard_map/jvp()/dot_general | solution.py:21
  105.3 0.0 copy-done.8
  105.3 13.7 %fusion.27 = bf16[1024,1024]{0,1:T(8,128)(2,1)S(1)} fusion(bf16[1024,3328]{1,0:T(8,128)(2,1)} %convolution_convert_fusion.4, bf16[2,1024,3328]{2,1,0:T(8,128)(2,1)} %param.14, f32[1024,3328]{1,0:T(8,128)} %get-tuple-element.29), kind=kOutput, calls=%fused_computation.51 | convolution fusion | flops 6999769088 | bytes 29360128 | tf_op jit(solution)/shard_map/transpose(jvp())/dot_general | solution.py:22
  119.0 0.0 copy-done.4
  119.0 0.0 copy-start.7
  119.0 14.4 %fusion.59 = bf16[1,1024,3328]{2,1,0:T(8,128)(2,1)} fusion(bf16[1024,3328]{1,0:T(8,128)(2,1)} %convolution_convert_fusion.4, bf16[1024,1024]{0,1:T(8,128)(2,1)S(1)} %copy-done.4, f32[1024]{0:T(1024)S(1)} %fusion.90, f32[1024,3328]{1,0:T(8,128)} %get-tuple-element.29), kind=kOutput, calls=%fused_computation.88 | convolution fusion | flops 7006322688 | bytes 29364224 | tf_op jit(solution)/shard_map/transpose(jvp())/dot_general | solution.py:22
  133.4 0.0 copy-done.7
  133.4 14.8 %fusion.54 = bf16[1,3328,1024]{2,1,0:T(8,128)(2,1)} fusion(f32[1024,3328]{1,0:T(8,128)} %fusion.33, bf16[1,1024,1024]{2,1,0:T(8,128)(2,1)S(1)} %copy-done.7, f32[1024,3328]{1,0:T(8,128)} %get-tuple-element.29), kind=kOutput, calls=%fused_computation.85 | convolution fusion | flops 7003176960 | bytes 36175872 | tf_op jit(solution)/shard_map/transpose(jvp())/dot_general | solution.py:10
  148.2 12.3 %fusion.52 = bf16[1,1024,3328]{2,1,0:T(8,128)(2,1)} fusion(bf16[1024,3328]{1,0:T(8,128)(2,1)} %get-tuple-element.28, bf16[1024,1024]{0,1:T(8,128)(2,1)S(1)} %copy-done.4, f32[1024]{0:T(1024)S(1)} %fusion.90), kind=kOutput, calls=%fused_computation.83 | convolution fusion | flops 6982467584 | bytes 15732736 | tf_op jit(solution)/shard_map/transpose(jvp())/dot_general | solution.py:21
  160.5 12.0 %fusion.72 = (f32[1024]{0:T(1024)S(1)}, bf16[1024,1024]{0,1:T(8,128)(2,1)S(1)}) fusion(bf16[1024,1024]{0,1:T(8,128)(2,1)S(1)} %copy-done.4, bf16[1024,1024]{0,1:T(8,128)(2,1)S(1)} %fusion.27, bf16[1024,3328]{1,0:T(8,128)(2,1)} %get-tuple-element.28, bf16[2,1024,3328]{2,1,0:T(8,128)(2,1)} %param.13), kind=kOutput, calls=%fused_computation.104 | convolution fusion | flops 6984563712 | bytes 19927040 | tf_op jit(solution)/shard_map/transpose(jvp())/dot_general | solution.py:21
  172.6 0.0 copy-done.9
  172.6 0.0 copy-done
  172.6 1.6 fusion.75
  174.2 0.0 copy-start.5
  174.2 1.3 copy-done.5
  175.5 0.0 slice-done
  175.5 0.0 slice-done.1
  175.5 0.0 slice-done.2
  175.5 0.0 slice-done.3
  175.5 9.4 %convolution_convert_fusion.3 = bf16[1024,3328]{1,0:T(8,128)(2,1)} fusion(bf16[1024,1024]{0,1:T(8,128)(2,1)S(1)} %fusion.75, bf16[2,3328,1024]{2,1,0:T(8,128)(2,1)S(1)} %bitcast.75), kind=kOutput, calls=%fused_computation.58 | convolution fusion | flops 6982729728 | bytes 15728640 | tf_op jit(solution)/shard_map/transpose(jvp())/dot_general | solution.py:10
  184.9 12.7 %fusion.53 = bf16[1,3328,1024]{2,1,0:T(8,128)(2,1)} fusion(bf16[1024,3328]{1,0:T(8,128)(2,1)} %get-tuple-element.24, bf16[1024,1024]{0,1:T(8,128)(2,1)} %copy-done.5), kind=kOutput, calls=%fused_computation.84 | convolution fusion | flops 6982729728 | bytes 15728640 | tf_op jit(solution)/shard_map/transpose(jvp())/dot_general | solution.py:10
  197.7 13.5 %fusion.55 = bf16[1,1024,3328]{2,1,0:T(8,128)(2,1)} fusion(bf16[1024,3328]{1,0:T(8,128)(2,1)S(1)} %copy-done.12, f32[1024,3328]{1,0:T(8,128)} %fusion.46, bf16[1,1024,1024]{1,2,0:T(8,128)(2,1)S(1)} %copy-done.2, f32[1024]{0:T(1024)S(1)} %copy-done.11), kind=kOutput, calls=%fused_computation.86 | convolution fusion | flops 7006322688 | bytes 29364224 | tf_op jit(solution)/shard_map/transpose(jvp())/dot_general | solution.py:22
  211.2 16.8 %fusion.56 = bf16[1,1024,3328]{2,1,0:T(8,128)(2,1)} fusion(f32[1024,3328]{1,0:T(8,128)} %fusion.46, f32[1024,3328]{1,0:T(8,128)} %get-tuple-element.25, bf16[1024,3328]{1,0:T(8,128)(2,1)} %convolution_convert_fusion.3, bf16[1,1024,1024]{1,2,0:T(8,128)(2,1)S(1)} %copy-done.2, f32[1024]{0:T(1024)S(1)} %copy-done.11), kind=kOutput, calls=%fused_computation.87 | convolution fusion | flops 7023362048 | bytes 42995712 | tf_op jit(solution)/shard_map/transpose(jvp())/dot_general | solution.py:21
  228.0 0.0 all-reduce.3.cloned.1.call-update
  228.0 303.5 %all-reduce.3.cloned.1.call-done = (bf16[1,1024,3328]{2,1,0:T(8,128)(2,1)}, bf16[1,1024,3328]{2,1,0:T(8,128)(2,1)}, bf16[1,1024,3328]{2,1,0:T(8,128)(2,1)}, bf16...) async-done(((bf16[1,1024,3328]{2,1,0:T(8,128)(2,1)}, bf16[1,1024,3328]{2,1,0:T(8,128)(2,1)}, ...) | async-done | bytes 40894480 | tf_op jit(solution)/shard_map/psum | solution.py:45
  531.6 51.3 %fusion.10 = (bf16[2,3328,1024]{2,1,0:T(8,128)(2,1)}, f32[2,3328,1024]{2,1,0:T(8,128)}, f32[2,3328,1024]{2,1,0:T(8,128)}) fusion(bf16[2,3328,1024]{2,1,0:T(8,128)(2,1)} %param.15, bf16[1,3328,1024]{2,1,0:T(8,128)(2,1)} %get-tuple-element.13, bf16[1,3328,1024]{2,1,0:T(8,128)(2,1)} %get-tuple-element.14, f32[2,3328,1024]{2,1,0:T(8,128)} %param.21, ...), kind=kLoop, calls=%fused_computation.22 | loop fusion | flops 129499136 | bytes 149946368 | tf_op jit(solution)/shard_map/convert_element_type | solution.py:30
  582.8 93.5 %fusion.2 = (bf16[2,1024,3328]{2,1,0:T(8,128)(2,1)}, f32[2,1024,3328]{2,1,0:T(8,128)}, f32[2,1024,3328]{2,1,0:T(8,128)}, bf16[2,1024,3328]{2,1,0:T(8,128)(2,1)},...) fusion(bf16[2,1024,3328]{2,1,0:T(8,128)(2,1)} %param.13, bf16[1,1024,3328]{2,1,0:T(8,128)(2,1)} %get-tuple-element.9, ...), kind=kLoop, calls=%fused_computation.14 | loop fusion | flops 258998272 | bytes 299892736 | tf_op jit(solution)/shard_map/convert_element_type | solution.py:30
  (23 shorter events, 0.1 us)
Async XLA Ops:
  7.2 524.4 %all-reduce.3.cloned.1.call-start = ((), (), s32[]{:S(2)}) async-start(), calls=%async_computation | async-start | bytes 81788928 | tf_op jit(solution)/shard_map/psum | solution.py:45
  10.1 44.5 %copy-start.1 = (bf16[1,1024,1024]{1,2,0:T(8,128)(2,1)}, bf16[1,1024,1024]{1,2,0:T(8,128)(2,1)S(1)}, u32[]{:S(2)}) copy-start(bf16[1,1024,1024]{1,2,0:T(8,128)(2,1)S(1)} %copy.20) | copy-start | bytes 6291460
  10.6 27.0 %copy-start.10 = (f32[1024]{0:T(1024)}, f32[1024]{0:T(1024)S(1)}, u32[]{:S(2)}) copy-start(f32[1024]{0:T(1024)S(1)} %add_rsqrt_fusion) | copy-start | bytes 12292
  10.6 16.8 %slice-start.4 = ((s8[13631488]{0:T(1024)(128)(4,1)}), s8[1048576]{0:T(1024)(128)(4,1)S(1)}, s32[]{:S(2)}) async-start(s8[13631488]{0:T(1024)(128)(4,1)} %bitcast.76), calls=%async_computation.5 | async-start | bytes 2097152
  14.8 12.7 %slice-start.5 = ((s8[13631488]{0:T(1024)(128)(4,1)}), s8[4194304]{0:T(1024)(128)(4,1)S(1)}, s32[]{:S(2)}) async-start(s8[13631488]{0:T(1024)(128)(4,1)} %bitcast.76), calls=%async_computation.6 | async-start | bytes 8388608
  14.8 12.7 %slice-start.6 = ((s8[13631488]{0:T(1024)(128)(4,1)}), s8[4194304]{0:T(1024)(128)(4,1)S(1)}, s32[]{:S(2)}) async-start(s8[13631488]{0:T(1024)(128)(4,1)} %bitcast.76), calls=%async_computation.7 | async-start | bytes 8388608
  14.8 12.7 %slice-start.7 = ((s8[13631488]{0:T(1024)(128)(4,1)}), s8[4194304]{0:T(1024)(128)(4,1)S(1)}, s32[]{:S(2)}) async-start(s8[13631488]{0:T(1024)(128)(4,1)} %bitcast.76), calls=%async_computation.8 | async-start | bytes 8388608
  14.8 12.7 %copy-start.6 = (bf16[1,1024,1024]{2,1,0:T(8,128)(2,1)S(1)}, bf16[1,1024,1024]{2,1,0:T(8,128)(2,1)}, u32[]{:S(2)}) copy-start(bf16[1,1024,1024]{2,1,0:T(8,128)(2,1)} %param.11) | copy-start | bytes 6291460
  66.5 1.3 copy-start.3
  66.5 38.7 %copy-start.8 = (f32[1024]{0:T(1024)}, f32[1024]{0:T(1024)S(1)}, u32[]{:S(2)}) copy-start(f32[1024]{0:T(1024)S(1)} %get-tuple-element.26) | copy-start | bytes 12292
  105.3 13.7 %copy-start.4 = (bf16[1024,1024]{0,1:T(8,128)(2,1)S(1)}, bf16[1024,1024]{0,1:T(8,128)(2,1)}, u32[]{:S(2)}) copy-start(bf16[1024,1024]{0,1:T(8,128)(2,1)} %copy-done.3) | copy-start | bytes 6291460
  119.0 14.4 %copy-start.7 = (bf16[1,1024,1024]{2,1,0:T(8,128)(2,1)S(1)}, bf16[1,1024,1024]{2,1,0:T(8,128)(2,1)}, u32[]{:S(2)}) copy-start(bf16[1,1024,1024]{2,1,0:T(8,128)(2,1)} %param.12) | copy-start | bytes 6291460
  148.2 27.2 %slice-start = ((s8[13631488]{0:T(1024)(128)(4,1)}), s8[4194304]{0:T(1024)(128)(4,1)S(1)}, s32[]{:S(2)}) async-start(s8[13631488]{0:T(1024)(128)(4,1)} %bitcast.74), calls=%async_computation.1 | async-start | bytes 8388608
  148.2 27.2 %slice-start.1 = ((s8[13631488]{0:T(1024)(128)(4,1)}), s8[4194304]{0:T(1024)(128)(4,1)S(1)}, s32[]{:S(2)}) async-start(s8[13631488]{0:T(1024)(128)(4,1)} %bitcast.74), calls=%async_computation.2 | async-start | bytes 8388608
  148.2 27.2 %slice-start.2 = ((s8[13631488]{0:T(1024)(128)(4,1)}), s8[4194304]{0:T(1024)(128)(4,1)S(1)}, s32[]{:S(2)}) async-start(s8[13631488]{0:T(1024)(128)(4,1)} %bitcast.74), calls=%async_computation.3 | async-start | bytes 8388608
  160.5 12.0 %copy-start.9 = (f32[1024]{0:T(1024)S(1)}, f32[1024]{0:T(1024)}, u32[]{:S(2)}) copy-start(f32[1024]{0:T(1024)} %copy-done.8) | copy-start | bytes 12292
  160.5 12.1 %copy-start = (bf16[1,1024,1024]{1,2,0:T(8,128)(2,1)S(1)}, bf16[1,1024,1024]{1,2,0:T(8,128)(2,1)}, u32[]{:S(2)}) copy-start(bf16[1,1024,1024]{1,2,0:T(8,128)(2,1)} %copy.21) | copy-start | bytes 6291460
  160.5 15.0 %slice-start.3 = ((s8[13631488]{0:T(1024)(128)(4,1)}), s8[1048576]{0:T(1024)(128)(4,1)S(1)}, s32[]{:S(2)}) async-start(s8[13631488]{0:T(1024)(128)(4,1)} %bitcast.74), calls=%async_computation.4 | async-start | bytes 2097152
  174.2 1.3 copy-start.5
  184.9 12.7 %copy-start.2 = (bf16[1,1024,1024]{1,2,0:T(8,128)(2,1)S(1)}, bf16[1,1024,1024]{1,2,0:T(8,128)(2,1)}, u32[]{:S(2)}) copy-start(bf16[1,1024,1024]{1,2,0:T(8,128)(2,1)} %copy-done.1) | copy-start | bytes 6291460
  184.9 12.7 %copy-start.11 = (f32[1024]{0:T(1024)S(1)}, f32[1024]{0:T(1024)}, u32[]{:S(2)}) copy-start(f32[1024]{0:T(1024)} %copy-done.10) | copy-start | bytes 12292
  184.9 12.7 %copy-start.12 = (bf16[1024,3328]{1,0:T(8,128)(2,1)S(1)}, bf16[1024,3328]{1,0:T(8,128)(2,1)}, u32[]{:S(2)}) copy-start(bf16[1024,3328]{1,0:T(8,128)(2,1)} %convolution_convert_fusion.3) | copy-start | bytes 20447236
Sparse Core Ops, SparseCore 0:
  228.2 303.3 all-reduce.2
where the time goes:
time: 692 us; the launch traced here: 683 us
  waiting for transfers between devices  304 us (44%)
  matrix products  209 us (30%)
  other arithmetic  147 us (21%)
  between operations  14.4 us (2%)
  local copies, waits for them, and re-layouts  9.72 us (1%)
    psum x1, waiting for transfers between devices, step(): summed[number] = [lax.psum(by_w[name], 'dp') for name in NAMES]  304 us
    convert_element_type x2, other arithmetic, adamw(): return ((w - 0.02 * step).astype(jnp.bfloat16), m, v)  145 us
    dot_general x5, matrix products, layer(): gate = jnp.dot(a, w['w_gate'], preferred_element_type=jnp.float32)  75.3 us
    dot_general x5, matrix products, layer(): up = jnp.dot(a, w['w_up'], preferred_element_type=jnp.float32)  72 us
    dot_general x5, matrix products, matmul(): jnp.dot(a, w, preferred_element_type=jnp.float32).astype(jnp.bfloat16)  61.5 us
  transfers between devices with their start and end apart: 1, of which 1 were waited for; matrix products, arithmetic and copies ran while one was open for 0% of the time, Pallas kernels for 0%

commit v1 on v0

v1 whole, which is shorter than its diff:
```python
import functools

import jax
import jax.numpy as jnp
from jax import lax
from jax.experimental import pallas as pl
from jax.experimental.pallas import tpu as pltpu
from jax.sharding import PartitionSpec as P

NAMES = ("w_gate", "w_up", "w_down")
MESH = pl.DeviceIdType.MESH
SIDE = 4
STRIDE = (32, 8, 2)
OFFSETS = (2, 1, 3)
D, FF, TOKENS = 1024, 3328, 1024
HALF = FF // 2
SLOTS = 4


def matmul(a, w):
    return jnp.dot(a, w, preferred_element_type=jnp.float32).astype(jnp.bfloat16)


def matmul_t(a, w):
    return lax.dot_general(a, w, (((1,), (1,)), ((), ())), preferred_element_type=jnp.float32).astype(jnp.bfloat16)


def normed(h):
    wide = h.astype(jnp.float32)
    scale = lax.rsqrt(jnp.mean(wide**2, -1, keepdims=True) + 1e-6)
    return (wide * scale).astype(jnp.bfloat16)


def exchange_kernel(l0, l1, l2, r0, r1, r2, out, lhs, rhs, mine, part, got_a, got_b, got_c, total, load, core_s, core_r, a_s, a_r, b_s, b_r, c_s, c_r):
    me = lax.axis_index("dp")
    core = lax.rem(me, 2)
    partner = me + 1 - 2 * core
    place = [lax.rem(lax.div(me, s), SIDE) for s in STRIDE]

    def to(device):
        return {"device_id": (0, device), "device_id_type": MESH}

    def along(axis, k):
        there = lax.rem(place[axis] + k, SIDE)
        return me + (there - place[axis]) * STRIDE[axis], there

    loads = []
    for n, (src, dst) in enumerate([(l2, lhs.at[2]), (r2, rhs.at[2]), (l0, lhs.at[0]), (r0, rhs.at[0]), (l1, lhs.at[1]), (r1, rhs.at[1])]):
        copy = pltpu.make_async_copy(src, dst, load.at[n])
        copy.start()
        loads.append(copy)
    barrier = pltpu.get_barrier_semaphore()
    pl.semaphore_signal(barrier, inc=1, **to(partner))
    for axis in range(3):
        for k in OFFSETS:
            pl.semaphore_signal(barrier, inc=1, **to(along(axis, k)[0]))
    pl.semaphore_wait(barrier, 10)

    def rows(index, size):
        return pl.ds(pl.multiple_of(index * size, size), size)

    order = (2, 0, 1)
    units = [(m, step) for step in range(4) for m in order]

    def block_of(m, step):
        return along(m, OFFSETS[step])[1] if step < 3 else place[m]

    def product(m, block, half):
        columns = pl.ds(pl.multiple_of(half * HALF, 128), HALF)
        return jnp.dot(lhs[m, rows(block, 256), :], rhs[m, :, columns], preferred_element_type=jnp.float32)

    core_copies, sends = [], []

    def give(n):
        m, step = units[n]
        if step == 0:
            loads[2 * order.index(m)].wait()
            loads[2 * order.index(m) + 1].wait()
        slot = n % SLOTS
        if n >= SLOTS:
            core_copies[n - SLOTS].wait_send()
        mine[slot] = product(m, block_of(m, step), 1 - core).astype(jnp.bfloat16)
        copy = pltpu.make_async_remote_copy(mine.at[slot], part.at[n], core_s.at[n], core_r.at[n], **to(partner))
        copy.start()
        core_copies.append(copy)

    ahead = 3
    for n in range(ahead):
        give(n)
    for n, (m, step) in enumerate(units):
        if n + ahead < len(units):
            give(n + ahead)
        own = product(m, block_of(m, step), core)
        core_copies[n].wait_recv()
        summed = own + part[n].astype(jnp.float32)
        if step < 3:
            part[n] = summed.astype(jnp.bfloat16)
            copy = pltpu.make_async_remote_copy(part.at[n], got_a.at[m, step], a_s.at[m, step], a_r.at[m, step], **to(along(m, OFFSETS[step])[0]))
            copy.start()
            sends.append((m, copy))
        else:
            total[m] = summed

    def level(axis_of, got_from, copies, size, buffer, got, s, r):
        following = []
        for m in order:
            for n, copy in copies:
                if n == m:
                    copy.wait_recv()
            summed = total[m, : 4 * size]
            for step in range(3):
                summed = summed + got_from[m, step].astype(jnp.float32)
            total[m, : 4 * size] = summed
            buffer[m] = summed.astype(jnp.bfloat16)
            axis = axis_of(m)
            for step in range(3):
                device, there = along(axis, OFFSETS[step])
                copy = pltpu.make_async_remote_copy(buffer.at[m, rows(there, size)], got.at[m, step], s.at[m, step], r.at[m, step], **to(device))
                copy.start()
                following.append((m, copy))
            kept = total[m, rows(place[axis], size), :]
            total[m, :size] = kept
        return following

    def second(m):
        return (m + 1) % 3

    def third(m):
        return (m + 2) % 3

    b_copies = level(second, got_a, sends, 64, got_b["send"], got_b["got"], b_s, b_r)
    c_copies = level(third, got_b["got"], b_copies, 16, got_c["send"], got_c["got"], c_s, c_r)
    for m in order:
        for n, copy in c_copies:
            if n == m:
                copy.wait_recv()
        summed = total[m, :16]
        for step in range(3):
            summed = summed + got_c["got"][m, step].astype(jnp.float32)
        out[:, m * HALF : (m + 1) * HALF] = summed.astype(jnp.bfloat16)
    for copy in core_copies[-SLOTS:]:
        copy.wait_send()
    for _, copy in sends + b_copies + c_copies:
        copy.wait_send()


def exchange(lhs, rhs, number):
    def dma(*shape):
        return pltpu.SemaphoreType.DMA(shape)

    bf16, f32 = jnp.bfloat16, jnp.float32
    return pl.pallas_call(
        exchange_kernel,
        out_shape=jax.ShapeDtypeStruct((16, 3 * HALF), bf16),
        in_specs=[pl.BlockSpec(memory_space=pl.ANY)] * 6,
        out_specs=pl.BlockSpec(memory_space=pltpu.VMEM),
        scratch_shapes=[
            pltpu.VMEM((3, D, TOKENS), bf16),
            pltpu.VMEM((3, TOKENS, FF), bf16),
            pltpu.VMEM((SLOTS, 256, HALF), bf16),
            pltpu.VMEM((12, 256, HALF), bf16),
            pltpu.VMEM((3, 3, 256, HALF), bf16),
            {"send": pltpu.VMEM((3, 256, HALF), bf16), "got": pltpu.VMEM((3, 3, 64, HALF), bf16)},
            {"send": pltpu.VMEM((3, 64, HALF), bf16), "got": pltpu.VMEM((3, 3, 16, HALF), bf16)},
            pltpu.VMEM((3, 256, HALF), f32),
            dma(6),
            dma(12),
            dma(12),
            *[dma(3, 3)] * 6,
        ],
        compiler_params=pltpu.CompilerParams(collective_id=number, has_side_effects=True, vmem_limit_bytes=67_043_328),
        cost_estimate=pl.CostEstimate(flops=6 * D * TOKENS * FF, bytes_accessed=26_000_000, transcendentals=0),
        name=f"exchange_{number}",
    )(*lhs, *rhs)


def update(w, m, v, g):
    m = 0.9 * m + 0.1 * g
    v = 0.95 * v + 0.05 * g * g
    step = m * lax.rsqrt(v + 1e-8) + 0.1 * w
    return w - 0.02 * step, m, v


def adamw_kernel(g, w, m, v, *rest):
    new_w, new_m, new_v = rest[-3:]
    for half in range(2):
        at = (0, slice(None), slice(half * HALF, (half + 1) * HALF))
        one = g[:, half].reshape(w.shape[1], HALF).astype(jnp.float32)
        a, b, c = update(w[at].astype(jnp.float32), m[at], v[at], one)
        new_w[at] = a.astype(jnp.bfloat16)
        new_m[at] = b
        new_v[at] = c


def adamw_down_kernel(g, w, m, v, *rest):
    new_w, new_m, new_v = rest[-3:]
    one = g[:, 0].reshape(D, 128).astype(jnp.float32).T
    a, b, c = update(w[0].astype(jnp.float32), m[0], v[0], one)
    new_w[0] = a.astype(jnp.bfloat16)
    new_m[0] = b
    new_v[0] = c


def adamw(which, layer, gathered, w, m, v, before):
    if which < 2:
        size = 64
        body, steps = adamw_kernel, D // size
        g_spec = pl.BlockSpec((size // 16, 2, 16, HALF), lambda i: (i, 0, 0, which))
        spec = pl.BlockSpec((1, size, FF), lambda i: (layer, i, 0))
    else:
        body, steps = adamw_down_kernel, FF // 128
        g_spec = pl.BlockSpec((64, 1, 16, 128), lambda i: (0, i // 13, 0, 26 + i % 13))
        spec = pl.BlockSpec((1, 128, D), lambda i: (layer, i, 0))
    more = [] if before is None else list(before)
    shapes = [jax.ShapeDtypeStruct(w.shape, t) for t in (jnp.bfloat16, jnp.float32, jnp.float32)]
    return pl.pallas_call(
        body,
        grid=(steps,),
        out_shape=shapes,
        in_specs=[g_spec, spec, spec, spec] + [pl.BlockSpec(memory_space=pl.ANY)] * len(more),
        out_specs=[spec] * 3,
        input_output_aliases={4 + i: i for i in range(len(more))},
        compiler_params=pltpu.CompilerParams(vmem_limit_bytes=50_000_000),
        cost_estimate=pl.CostEstimate(flops=20 * D * FF, bytes_accessed=22 * D * FF, transcendentals=D * FF),
        name=f"adamw_{which}_{layer}",
    )(gathered, w, m, v, *more)


def by_owner(t, first):
    blocks = t.reshape(SIDE, SIDE, SIDE, 16, t.shape[1])
    order = [(first + i) % 3 for i in range(3)]
    return blocks.transpose(*order, 3, 4).reshape(t.shape)


def solution(mesh):
    def step(x, dy, *arrays):
        weights, m, v = (arrays[i : i + 3] for i in (0, 3, 6))
        layers = weights[0].shape[0]
        w_gate, w_up, w_down = weights
        h, kept = x[0], []
        for n in range(layers):
            a, back = jax.vjp(normed, h)
            gate = jnp.dot(a, w_gate[n], preferred_element_type=jnp.float32)
            up = jnp.dot(a, w_up[n], preferred_element_type=jnp.float32)
            hidden = (jax.nn.silu(gate) * up).astype(jnp.bfloat16)
            kept.append((a, back, gate, up, hidden))
            if n < layers - 1:
                h = h + matmul(hidden, w_down[n])
        by_h, gathered = dy[0], [None] * layers
        for n in reversed(range(layers)):
            a, back, gate, up, hidden = kept[n]
            by_hidden = matmul_t(by_h, w_down[n]).astype(jnp.float32)
            sig = jax.nn.sigmoid(gate)
            silu = gate * sig
            by_up = (by_hidden * silu).astype(jnp.bfloat16)
            by_gate = (by_hidden * up * (sig + silu * (1 - sig))).astype(jnp.bfloat16)
            a_t, by_h_t = a.T, by_h.T
            lhs = [by_owner(a_t, 0), by_owner(a_t, 1), by_owner(by_h_t, 2)]
            chunk = exchange(lhs, [by_gate, by_up, hidden], n)
            gathered[n] = lax.all_gather(chunk, "dp", axis=0, tiled=False).reshape(64, 2, 16, 3 * HALF)
            if n:
                (by_in,) = back(matmul_t(by_gate, w_gate[n]) + matmul_t(by_up, w_up[n]))
                by_h = by_h + by_in
        new = [None] * 3
        for n in reversed(range(layers)):
            new = [adamw(i, n, gathered[n], weights[i], m[i], v[i], new[i]) for i in range(3)]
        return tuple(one[which] for which in range(3) for one in new)

    return jax.shard_map(
        step,
        mesh=mesh,
        in_specs=(P(("rep", "dp"), None, None),) * 2 + (P(None, None, None),) * 9,
        out_specs=(P("rep", None, None),) * 9,
        check_vma=False,
    )
```

time: 692 us -> 534 us (0.77)
  Pallas kernels: 0 us -> 357 us
  waiting for transfers between devices: 304 us -> 0.07 us
  other arithmetic: 147 us -> 11.9 us
  matrix products: 209 us -> 127 us
    pallas_call x0 -> x8, Pallas kernels: none -> 357 us  [the longest x6 191 us: adamw(): pl.pallas_call(body, grid=(steps,), out_shape=shapes, in_specs=[g_spec, s...]
    psum x1 -> x0, waiting for transfers between devices: 304 us -> none  [step(): summed[number] = [lax.psum(by_w[name], 'dp') for name in NAMES]]
    convert_element_type x2, other arithmetic: 145 us -> 4.48 us  [normed(): return (wide * scale).astype(jnp.bfloat16)]
    dot_general x5 -> x1, matrix products: 61.5 us -> 13 us  [matmul(): jnp.dot(a, w, preferred_element_type=jnp.float32).astype(jnp.bfloat16)]
    dot_general x10 -> x8, matrix products: 147 us -> 114 us  [the longest x4 54.5 us: matmul_t(): lax.dot_general(a, w, (((1,), (1,)), ((), ())), preferred_element_type=jn...]
  transfers between devices with their start and end apart: 1 -> 2, of which waited for: 1 -> 0; matrix products, arithmetic and copies ran while one was open for 0% -> 10% of each run, Pallas kernels for 0% -> 35%
where the time goes in v1:
time: 534 us; the launch traced here: 525 us
  Pallas kernels  357 us (67%)
  matrix products  127 us (24%)
  between operations  14.8 us (3%)
  local copies, waits for them, and re-layouts  13.7 us (3%)
  other arithmetic  11.9 us (2%)
    pallas_call x6, Pallas kernels, adamw(): pl.pallas_call(body, grid=(steps,), out_shape=shapes, in_specs=[g_spec, s...  191 us
    pallas_call x2, Pallas kernels, exchange(): pl.pallas_call(exchange_kernel, out_shape=jax.ShapeDtypeStruct((16, 3 * H...  166 us
    dot_general x4, matrix products, matmul_t(): lax.dot_general(a, w, (((1,), (1,)), ((), ())), preferred_element_type=jn...  54.5 us
    dot_general x2, matrix products, step(): up = jnp.dot(a, w_up[n], preferred_element_type=jnp.float32)  38.8 us
    dot_general x2, matrix products, step(): gate = jnp.dot(a, w_gate[n], preferred_element_type=jnp.float32)  20.8 us
    dot_general x1, matrix products, matmul(): jnp.dot(a, w, preferred_element_type=jnp.float32).astype(jnp.bfloat16)  13 us
  transfers between devices with their start and end apart: 2, of which 0 were waited for; matrix products, arithmetic and copies ran while one was open for 10% of the time, Pallas kernels for 35%

profile of v1, /device:TPU:0, one launch (start us, length us, event | category | flops | bytes accessed | tf_op | source)
XLA Modules:
  0.0 524.7 jit_solution(14611307705145270344)
XLA Ops:
  7.2 0.0 all-gather.7.cloned.1.call-start
  7.2 2.9 copy.29
  10.1 0.0 copy-start
  10.1 0.5 fusion.33
  10.6 0.0 slice-start.4
  10.6 4.2 copy.31
  14.8 12.6 %convolution_convert_fusion.1 = bf16[1024,3328]{1,0:T(8,128)(2,1)} fusion(bf16[2,3328,1024]{2,1,0:T(8,128)(2,1)} %w.11, bf16[1,1024,1024]{2,1,0:T(8,128)(2,1)} %param.12), kind=kOutput, calls=%fused_computation.17 | convolution fusion | flops 6982729728 | bytes 15728640 | tf_op jit(solution)/shard_map/dot_general | solution.py:25
  27.4 0.0 slice-done.4
  27.5 10.1 %fusion.21 = f32[1024,3328]{1,0:T(8,128)} fusion(bf16[2,1024,3328]{2,1,0:T(8,128)(2,1)S(1)} %bitcast.99, bf16[1,1024,1024]{2,1,0:T(8,128)(2,1)S(1)} %copy-done.5, f32[1024]{0:T(1024)S(1)} %add_rsqrt_fusion), kind=kOutput, calls=%fused_computation.35 | convolution fusion | flops 6982467584 | bytes 22548480 | tf_op jit(solution)/shard_map/dot_general | solution.py:243
  37.6 17.0 %multiply_convert_fusion.1 = (bf16[1024,3328]{1,0:T(8,128)(2,1)}, f32[1024,3328]{1,0:T(8,128)}) fusion(f32[1024,3328]{1,0:T(8,128)} %fusion.21, bf16[2,1024,3328]{2,1,0:T(8,128)(2,1)} %w.9, bf16[1,1024,1024]{2,1,0:T(8,128)(2,1)} %param.11, f32[1024]{0:T(1024)S(1)} %add_rsqrt_fusion), kind=kOutput, calls=%fused_computation.12 | convolution fusion | flops 7002914816 | bytes 42995712 | tf_op jit(solution)/shard_map/dot_general | solution.py:244
  54.6 0.0 slice-start.9
  54.6 0.0 slice-start.10
  54.6 0.0 slice-start.11
  54.6 13.0 %fusion.37 = (f32[1024]{0:T(1024)S(1)}, bf16[1024,1024]{0,1:T(8,128)(2,1)}) fusion(bf16[1024,3328]{1,0:T(8,128)(2,1)} %get-tuple-element.50.r2, bf16[2,3328,1024]{2,1,0:T(8,128)(2,1)} %w.11, bf16[1,1024,1024]{1,2,0:T(8,128)(2,1)S(1)} %copy.29), kind=kOutput, calls=%fused_computation.54 | convolution fusion | flops 6984563712 | bytes 17829888 | tf_op jit(solution)/shard_map/dot_general | solution.py:21
  67.6 0.6 copy-done.10
  68.2 2.2 fusion.38
  70.4 3.5 fusion.56.l0
  73.9 1.5 copy.34
  75.4 0.0 slice-done.8
  75.4 0.0 slice-done.10
  75.4 10.7 %fusion.10 = f32[1024,3328]{1,0:T(8,128)} fusion(bf16[1024,1024]{0,1:T(8,128)(2,1)S(1)} %fusion.38, bf16[2,1024,3328]{2,1,0:T(8,128)(2,1)S(1)} %bitcast.101), kind=kOutput, calls=%fused_computation.24 | convolution fusion | flops 6979321856 | bytes 22544384 | tf_op jit(solution)/shard_map/dot_general | solution.py:243
  86.1 1.5 copy.33
  87.7 21.8 %multiply_convert_fusion = (bf16[1024,3328]{1,0:T(8,128)(2,1)}, bf16[1024,3328]{1,0:T(8,128)(2,1)}, bf16[1024,3328]{1,0:T(8,128)(2,1)}) fusion(f32[1024,3328]{1,0:T(8,128)} %fusion.10, bf16[1024,3328]{1,0:T(8,128)(2,1)} %convolution_convert_fusion.1, bf16[1024,1024]{0,1:T(8,128)(2,1)S(1)} %fusion.38, bf16[2,1024,3328]{2,1,0:T(8,128)(2,1)} %w.9), kind=kOutput, calls=%fused_computation.10 | convolution fusion | flops 7030439936 | bytes 49807360 | tf_op jit(solution)/shard_map/dot_general | solution.py:244
  109.5 80.1 %exchange_1.1 = bf16[16,4992]{1,0:T(8,128)(2,1)} custom-call(bf16[1024,1024]{1,0:T(8,128)(2,1)} %fusion.56.l0, bf16[1024,1024]{1,0:T(8,128)(2,1)} %bitcast.109, bf16[1024,1024]{1,0:T(8,128)(2,1)} %bitcast.108, bf16[1024,3328]{1,0:T(8,128)(2,1)} %get-tuple-element.46.r0, bf16[1024,3328]{1,0:T(8,128)(2,1)} %get-tuple-element.47.r1, ...), custom_call_target="tpu_custom_call" | custom-call | flops 20937965568 | bytes 26000000 | tf_op jit(solution)/shard_map/exchange_1/pallas_call | solution.py:152
  189.6 0.0 all-gather.7.cloned.1.call-update
  189.7 0.0 all-gather.5.cloned.1.call-start
  189.7 0.0 slice-start
  189.7 2.3 fusion.34
  192.0 1.5 copy.30
  193.5 11.6 %fusion.8 = bf16[1024,1024]{0,1:T(8,128)(2,1)S(1)} fusion(bf16[1024,3328]{1,0:T(8,128)(2,1)} %get-tuple-element.46.r0, bf16[2,1024,3328]{2,1,0:T(8,128)(2,1)} %w.7), kind=kOutput, calls=%fused_computation.22 | convolution fusion | flops 6979321856 | bytes 15728640 | tf_op jit(solution)/shard_map/dot_general | solution.py:25
  205.2 0.0 copy-start.11
  205.2 0.0 copy-start.4
  205.2 9.8 %fusion.39 = (f32[1024]{0:T(1024)S(1)}, bf16[1024,1024]{0,1:T(8,128)(2,1)S(1)}) fusion(bf16[1024,1024]{0,1:T(8,128)(2,1)S(1)} %copy-done.2, bf16[1024,1024]{0,1:T(8,128)(2,1)S(1)} %fusion.8, bf16[1024,3328]{1,0:T(8,128)(2,1)} %get-tuple-element.47.r1, bf16[2,1024,3328]{2,1,0:T(8,128)(2,1)S(1)} %bitcast.97), kind=kOutput, calls=%fused_computation.56 | convolution fusion | flops 6985612288 | bytes 19927040 | tf_op jit(solution)/shard_map/dot_general | solution.py:25
  215.0 0.0 copy-start.1
  215.1 1.6 fusion.41
  216.7 1.5 copy.32
  218.2 1.9 fusion.57.l0
  220.1 20.5 %fusion.5 = (bf16[1024,3328]{1,0:T(8,128)(2,1)}, bf16[1024,3328]{1,0:T(8,128)(2,1)}) fusion(f32[1024,3328]{1,0:T(8,128)} %fusion.21, f32[1024,3328]{1,0:T(8,128)} %get-tuple-element.51, bf16[1024,1024]{0,1:T(8,128)(2,1)S(1)} %fusion.41, bf16[2,3328,1024]{2,1,0:T(8,128)(2,1)} %w.11), kind=kOutput, calls=%fused_computation.9 | convolution fusion | flops 7027032064 | bytes 49807360 | tf_op jit(solution)/shard_map/dot_general | solution.py:25
  240.5 85.7 %exchange_0.1 = bf16[16,4992]{1,0:T(8,128)(2,1)} custom-call(bf16[1024,1024]{1,0:T(8,128)(2,1)} %fusion.57.l0, bf16[1024,1024]{1,0:T(8,128)(2,1)} %bitcast.106, bf16[1024,1024]{1,0:T(8,128)(2,1)} %bitcast.107, bf16[1024,3328]{1,0:T(8,128)(2,1)} %get-tuple-element.49.r0, bf16[1024,3328]{1,0:T(8,128)(2,1)} %get-tuple-element.48.r1, ...), custom_call_target="tpu_custom_call" | custom-call | flops 20937965568 | bytes 26000000 | tf_op jit(solution)/shard_map/exchange_0/pallas_call | solution.py:152
  326.2 0.0 all-gather.5.cloned.1.call-update
  326.2 0.0 all-gather.7.cloned.1.call-done
  326.2 35.6 %adamw_2_1.1 = (bf16[2,3328,1024]{2,1,0:T(8,128)(2,1)}, f32[2,3328,1024]{2,1,0:T(8,128)}, f32[2,3328,1024]{2,1,0:T(8,128)}) custom-call(bf16[64,2,16,4992]{3,2,1,0:T(8,128)(2,1)} %bitcast.90, bf16[2,3328,1024]{2,1,0:T(8,128)(2,1)} %w.11, f32[2,3328,1024]{2,1,0:T(8,128)} %m.11, f32[2,3328,1024]{2,1,0:T(8,128)} %v.11), custom_call_target="tpu_custom_call" | custom-call | flops 68157440 | bytes 74973184 | tf_op jit(solution)/shard_map/adamw_2_1/pallas_call | solution.py:216
  361.8 30.0 %adamw_1_1.1 = (bf16[2,1024,3328]{2,1,0:T(8,128)(2,1)}, f32[2,1024,3328]{2,1,0:T(8,128)}, f32[2,1024,3328]{2,1,0:T(8,128)}) custom-call(bf16[64,2,16,4992]{3,2,1,0:T(8,128)(2,1)} %bitcast.91, bf16[2,1024,3328]{2,1,0:T(8,128)(2,1)} %w.9, f32[2,1024,3328]{2,1,0:T(8,128)} %m.9, f32[2,1024,3328]{2,1,0:T(8,128)} %v.9), custom_call_target="tpu_custom_call" | custom-call | flops 68157440 | bytes 74973184 | tf_op jit(solution)/shard_map/adamw_1_1/pallas_call | solution.py:216
  391.8 30.0 %adamw_0_1.1 = (bf16[2,1024,3328]{2,1,0:T(8,128)(2,1)}, f32[2,1024,3328]{2,1,0:T(8,128)}, f32[2,1024,3328]{2,1,0:T(8,128)}) custom-call(bf16[64,2,16,4992]{3,2,1,0:T(8,128)(2,1)} %bitcast.92, bf16[2,1024,3328]{2,1,0:T(8,128)(2,1)} %w.7, f32[2,1024,3328]{2,1,0:T(8,128)} %m.7, f32[2,1024,3328]{2,1,0:T(8,128)} %v.7), custom_call_target="tpu_custom_call" | custom-call | flops 68157440 | bytes 74973184 | tf_op jit(solution)/shard_map/adamw_0_1/pallas_call | solution.py:216
  421.8 0.0 all-gather.5.cloned.1.call-done
  421.9 35.6 %adamw_2_0.1 = (bf16[2,3328,1024]{2,1,0:T(8,128)(2,1)}, f32[2,3328,1024]{2,1,0:T(8,128)}, f32[2,3328,1024]{2,1,0:T(8,128)}) custom-call(bf16[64,2,16,4992]{3,2,1,0:T(8,128)(2,1)} %bitcast.93, bf16[2,3328,1024]{2,1,0:T(8,128)(2,1)} %w.11, f32[2,3328,1024]{2,1,0:T(8,128)} %m.11, ...), custom_call_target="tpu_custom_call", output_to_operand_aliasing={{0}: (4, {}), {1}: (5, {}), {2}: (6, {})} | custom-call | flops 68157440 | bytes 74973184 | tf_op jit(solution)/shard_map/adamw_2_0/pallas_call | solution.py:216
  457.4 30.0 %adamw_1_0.1 = (bf16[2,1024,3328]{2,1,0:T(8,128)(2,1)}, f32[2,1024,3328]{2,1,0:T(8,128)}, f32[2,1024,3328]{2,1,0:T(8,128)}) custom-call(bf16[64,2,16,4992]{3,2,1,0:T(8,128)(2,1)} %bitcast.94, bf16[2,1024,3328]{2,1,0:T(8,128)(2,1)} %w.9, f32[2,1024,3328]{2,1,0:T(8,128)} %m.9, ...), custom_call_target="tpu_custom_call", output_to_operand_aliasing={{0}: (4, {}), {1}: (5, {}), {2}: (6, {})} | custom-call | flops 68157440 | bytes 74973184 | tf_op jit(solution)/shard_map/adamw_1_0/pallas_call | solution.py:216
  487.4 30.0 %adamw_0_0.1 = (bf16[2,1024,3328]{2,1,0:T(8,128)(2,1)}, f32[2,1024,3328]{2,1,0:T(8,128)}, f32[2,1024,3328]{2,1,0:T(8,128)}) custom-call(bf16[64,2,16,4992]{3,2,1,0:T(8,128)(2,1)} %bitcast.95, bf16[2,1024,3328]{2,1,0:T(8,128)(2,1)} %w.7, f32[2,1024,3328]{2,1,0:T(8,128)} %m.7, ...), custom_call_target="tpu_custom_call", output_to_operand_aliasing={{0}: (4, {}), {1}: (5, {}), {2}: (6, {})} | custom-call | flops 68157440 | bytes 74973184 | tf_op jit(solution)/shard_map/adamw_0_0/pallas_call | solution.py:216
  (41 shorter events, 0.1 us)
Async XLA Ops:
  7.2 319.1 %all-gather.7.cloned.1.call-start = ((), (), s32[]{:S(2)}) async-start(), calls=%async_computation.1 | async-start | bytes 20606976 | tf_op jit(solution)/shard_map/all_gather | solution.py:260
  10.1 44.5 %copy-start = (bf16[1,1024,1024]{1,2,0:T(8,128)(2,1)}, bf16[1,1024,1024]{1,2,0:T(8,128)(2,1)S(1)}, u32[]{:S(2)}) copy-start(bf16[1,1024,1024]{1,2,0:T(8,128)(2,1)S(1)} %copy.29) | copy-start | bytes 6291460
  10.6 27.0 %copy-start.8 = (f32[1024]{0:T(1024)}, f32[1024]{0:T(1024)S(1)}, u32[]{:S(2)}) copy-start(f32[1024]{0:T(1024)S(1)} %add_rsqrt_fusion) | copy-start | bytes 12292
  10.6 16.9 %slice-start.4 = ((s8[13631488]{0:T(1024)(128)(4,1)}), s8[1048576]{0:T(1024)(128)(4,1)S(1)}, s32[]{:S(2)}) async-start(s8[13631488]{0:T(1024)(128)(4,1)} %bitcast.98), calls=%async_computation.6 | async-start | bytes 2097152
  14.8 12.7 %slice-start.5 = ((s8[13631488]{0:T(1024)(128)(4,1)}), s8[4194304]{0:T(1024)(128)(4,1)S(1)}, s32[]{:S(2)}) async-start(s8[13631488]{0:T(1024)(128)(4,1)} %bitcast.98), calls=%async_computation.7 | async-start | bytes 8388608
  14.8 12.7 %slice-start.6 = ((s8[13631488]{0:T(1024)(128)(4,1)}), s8[4194304]{0:T(1024)(128)(4,1)S(1)}, s32[]{:S(2)}) async-start(s8[13631488]{0:T(1024)(128)(4,1)} %bitcast.98), calls=%async_computation.8 | async-start | bytes 8388608
  14.8 12.7 %slice-start.7 = ((s8[13631488]{0:T(1024)(128)(4,1)}), s8[4194304]{0:T(1024)(128)(4,1)S(1)}, s32[]{:S(2)}) async-start(s8[13631488]{0:T(1024)(128)(4,1)} %bitcast.98), calls=%async_computation.9 | async-start | bytes 8388608
  14.8 12.7 %copy-start.5 = (bf16[1,1024,1024]{2,1,0:T(8,128)(2,1)S(1)}, bf16[1,1024,1024]{2,1,0:T(8,128)(2,1)}, u32[]{:S(2)}) copy-start(bf16[1,1024,1024]{2,1,0:T(8,128)(2,1)} %param.11) | copy-start | bytes 6291460
  54.6 20.8 %slice-start.8 = ((s8[13631488]{0:T(1024)(128)(4,1)}), s8[4194304]{0:T(1024)(128)(4,1)S(1)}, s32[]{:S(2)}) async-start(s8[13631488]{0:T(1024)(128)(4,1)} %bitcast.100), calls=%async_computation.10 | async-start | bytes 8388608
  54.6 20.8 %slice-start.9 = ((s8[13631488]{0:T(1024)(128)(4,1)}), s8[4194304]{0:T(1024)(128)(4,1)S(1)}, s32[]{:S(2)}) async-start(s8[13631488]{0:T(1024)(128)(4,1)} %bitcast.100), calls=%async_computation.11 | async-start | bytes 8388608
  54.6 20.8 %slice-start.10 = ((s8[13631488]{0:T(1024)(128)(4,1)}), s8[4194304]{0:T(1024)(128)(4,1)S(1)}, s32[]{:S(2)}) async-start(s8[13631488]{0:T(1024)(128)(4,1)} %bitcast.100), calls=%async_computation.12 | async-start | bytes 8388608
  54.6 20.8 %slice-start.11 = ((s8[13631488]{0:T(1024)(128)(4,1)}), s8[1048576]{0:T(1024)(128)(4,1)S(1)}, s32[]{:S(2)}) async-start(s8[13631488]{0:T(1024)(128)(4,1)} %bitcast.100), calls=%async_computation.13 | async-start | bytes 2097152
  67.6 0.6 copy-start.10
  67.6 6.3 %copy-start.3 = (bf16[1,1024,1024]{1,2,0:T(8,128)(2,1)S(1)}, bf16[1,1024,1024]{1,2,0:T(8,128)(2,1)}, u32[]{:S(2)}) copy-start(bf16[1,1024,1024]{1,2,0:T(8,128)(2,1)} %copy.31) | copy-start | bytes 6291460
  68.2 2.2 copy-start.6
  189.7 232.2 %all-gather.5.cloned.1.call-start = ((), (), s32[]{:S(2)}) async-start(), calls=%async_computation | async-start | bytes 20606976 | tf_op jit(solution)/shard_map/all_gather | solution.py:260
  189.7 15.4 %slice-start = ((s8[13631488]{0:T(1024)(128)(4,1)}), s8[4194304]{0:T(1024)(128)(4,1)S(1)}, s32[]{:S(2)}) async-start(s8[13631488]{0:T(1024)(128)(4,1)} %bitcast.96), calls=%async_computation.2 | async-start | bytes 8388608
  193.5 11.6 %slice-start.1 = ((s8[13631488]{0:T(1024)(128)(4,1)}), s8[4194304]{0:T(1024)(128)(4,1)S(1)}, s32[]{:S(2)}) async-start(s8[13631488]{0:T(1024)(128)(4,1)} %bitcast.96), calls=%async_computation.3 | async-start | bytes 8388608
  193.5 11.6 %slice-start.2 = ((s8[13631488]{0:T(1024)(128)(4,1)}), s8[4194304]{0:T(1024)(128)(4,1)S(1)}, s32[]{:S(2)}) async-start(s8[13631488]{0:T(1024)(128)(4,1)} %bitcast.96), calls=%async_computation.4 | async-start | bytes 8388608
  193.5 11.6 %slice-start.3 = ((s8[13631488]{0:T(1024)(128)(4,1)}), s8[1048576]{0:T(1024)(128)(4,1)S(1)}, s32[]{:S(2)}) async-start(s8[13631488]{0:T(1024)(128)(4,1)} %bitcast.96), calls=%async_computation.5 | async-start | bytes 2097152
  193.5 11.6 %copy-start.2 = (bf16[1024,1024]{0,1:T(8,128)(2,1)S(1)}, bf16[1024,1024]{0,1:T(8,128)(2,1)}, u32[]{:S(2)}) copy-start(bf16[1024,1024]{0,1:T(8,128)(2,1)} %get-tuple-element.53) | copy-start | bytes 6291460
  205.2 9.9 %copy-start.11 = (f32[1024]{0:T(1024)S(1)}, f32[1024]{0:T(1024)}, u32[]{:S(2)}) copy-start(f32[1024]{0:T(1024)} %copy-done.10) | copy-start | bytes 12292
  205.2 9.9 %copy-start.4 = (bf16[1,1024,1024]{1,2,0:T(8,128)(2,1)S(1)}, bf16[1,1024,1024]{1,2,0:T(8,128)(2,1)}, u32[]{:S(2)}) copy-start(bf16[1,1024,1024]{1,2,0:T(8,128)(2,1)} %copy.31) | copy-start | bytes 6291460
  205.2 9.9 %copy-start.7 = (f32[1024]{0:T(1024)S(1)}, f32[1024]{0:T(1024)}, u32[]{:S(2)}) copy-start(f32[1024]{0:T(1024)} %copy-done.6) | copy-start | bytes 12292
  215.0 3.1 copy-start.1
  215.0 3.1 copy-start.9
Sparse Core Ops, SparseCore 0:
  189.8 111.6 all-gather.6
  326.3 82.5 all-gather.4

commit v2 on v1

--- a/solution.py
+++ b/solution.py
@@ -1,5 +1,3 @@
-import functools
-
 import jax
 import jax.numpy as jnp
 from jax import lax
@@ -17,18 +15,111 @@
 SLOTS = 4
 
 
-def matmul(a, w):
-    return jnp.dot(a, w, preferred_element_type=jnp.float32).astype(jnp.bfloat16)
-
-
-def matmul_t(a, w):
-    return lax.dot_general(a, w, (((1,), (1,)), ((), ())), preferred_element_type=jnp.float32).astype(jnp.bfloat16)
+def scale_of(wide):
+    return lax.rsqrt(jnp.mean(wide**2, -1, keepdims=True) + 1e-6)
 
 
 def normed(h):
     wide = h.astype(jnp.float32)
-    scale = lax.rsqrt(jnp.mean(wide**2, -1, keepdims=True) + 1e-6)
-    return (wide * scale).astype(jnp.bfloat16)
+    return (wide * scale_of(wide)).astype(jnp.bfloat16)
+
+
+def dot(a, w):
+    return jnp.dot(a, w, preferred_element_type=jnp.float32)
+
+
+def dot_t(a, w):
+    return lax.dot_general(a, w, (((1,), (1,)), ((), ())), preferred_element_type=jnp.float32)
+
+
+def add_up(total, term):
+    first = pl.program_id(0) == 0
+
+    @pl.when(first)
+    def _():
+        total[...] = term
+
+    @pl.when(jnp.logical_not(first))
+    def _():
+        total[...] += term
+
+
+def last():
+    return pl.program_id(0) == pl.num_programs(0) - 1
+
+
+def forward_kernel(h, a, w_gate, w_up, w_down, gate, up, hidden, next_h, next_a, total):
+    gate[...] = dot(a[...], w_gate[0])
+    up[...] = dot(a[...], w_up[0])
+    hidden[...] = (jax.nn.silu(gate[...]) * up[...]).astype(jnp.bfloat16)
+    add_up(total, dot(hidden[...], w_down[0]))
+
+    @pl.when(last())
+    def _():
+        out = h[...] + total[...].astype(jnp.bfloat16)
+        next_h[...] = out
+        next_a[...] = normed(out)
+
+
+def by_gate_and_up(gate, up, by_hidden):
+    by_hidden = by_hidden.astype(jnp.bfloat16).astype(jnp.float32)
+    sig = jax.nn.sigmoid(gate)
+    silu = gate * sig
+    by_up = (by_hidden * silu).astype(jnp.bfloat16)
+    by_gate = (by_hidden * up * (sig + silu * (1 - sig))).astype(jnp.bfloat16)
+    return silu, by_gate, by_up
+
+
+def last_layer_kernel(by_h, a, w_gate, w_up, w_down, hidden, by_gate, by_up):
+    gate, up = dot(a[...], w_gate[0]), dot(a[...], w_up[0])
+    silu, by_gate[...], by_up[...] = by_gate_and_up(gate, up, dot_t(by_h[...], w_down[0]))
+    hidden[...] = (silu * up).astype(jnp.bfloat16)
+
+
+def backward_kernel(by_h, w_down, gate, up, by_gate, by_up):
+    _, by_gate[...], by_up[...] = by_gate_and_up(gate[...], up[...], dot_t(by_h[...], w_down[0]))
+
+
+def by_input_kernel(h, by_h, by_gate, by_up, w_gate, w_up, by_in, total_gate, total_up):
+    add_up(total_gate, dot_t(by_gate[...], w_gate[0]))
+    add_up(total_up, dot_t(by_up[...], w_up[0]))
+
+    @pl.when(last())
+    def _():
+        by_a = (total_gate[...].astype(jnp.bfloat16) + total_up[...].astype(jnp.bfloat16)).astype(jnp.float32)
+        wide = h[...].astype(jnp.float32)
+        scale = scale_of(wide)
+        shared = jnp.sum(by_a * wide, -1, keepdims=True) * scale**3 / D
+        by_in[...] = by_h[...] + (by_a * scale - wide * shared).astype(jnp.bfloat16)
+
+
+TILE = 256
+
+
+def over_hidden(body, name, layer, kinds, out_kinds, totals, matmuls, *args):
+    specs = {
+        "s": pl.BlockSpec((TOKENS, D), lambda j: (0, 0)),
+        "r": pl.BlockSpec((1, TILE, D), lambda j: (layer, j, 0)),
+        "c": pl.BlockSpec((1, D, TILE), lambda j: (layer, 0, j)),
+        "t": pl.BlockSpec((TOKENS, TILE), lambda j: (0, j)),
+        "f": pl.BlockSpec((TOKENS, TILE), lambda j: (0, j)),
+    }
+    shapes = {
+        "s": jax.ShapeDtypeStruct((TOKENS, D), jnp.bfloat16),
+        "t": jax.ShapeDtypeStruct((TOKENS, FF), jnp.bfloat16),
+        "f": jax.ShapeDtypeStruct((TOKENS, FF), jnp.float32),
+    }
+    return pl.pallas_call(
+        body,
+        grid=(FF // TILE,),
+        in_specs=[specs[k] for k in kinds],
+        out_specs=[specs[k] for k in out_kinds],
+        out_shape=[shapes[k] for k in out_kinds],
+        scratch_shapes=[pltpu.VMEM((TOKENS, D), jnp.float32)] * totals,
+        compiler_params=pltpu.CompilerParams(vmem_limit_bytes=60_000_000),
+        cost_estimate=pl.CostEstimate(flops=2 * matmuls * TOKENS * D * FF, bytes_accessed=40_000_000, transcendentals=TOKENS * FF),
+        name=name,
+    )(*args)
 
 
 def exchange_kernel(l0, l1, l2, r0, r1, r2, out, lhs, rhs, mine, part, got_a, got_b, got_c, total, load, core_s, core_r, a_s, a_r, b_s, b_r, c_s, c_r):
@@ -181,49 +272,59 @@
     return w - 0.02 * step, m, v
 
 
-def adamw_kernel(g, w, m, v, *rest):
-    new_w, new_m, new_v = rest[-3:]
-    for half in range(2):
-        at = (0, slice(None), slice(half * HALF, (half + 1) * HALF))
-        one = g[:, half].reshape(w.shape[1], HALF).astype(jnp.float32)
-        a, b, c = update(w[at].astype(jnp.float32), m[at], v[at], one)
-        new_w[at] = a.astype(jnp.bfloat16)
-        new_m[at] = b
-        new_v[at] = c
-
-
-def adamw_down_kernel(g, w, m, v, *rest):
-    new_w, new_m, new_v = rest[-3:]
-    one = g[:, 0].reshape(D, 128).astype(jnp.float32).T
-    a, b, c = update(w[0].astype(jnp.float32), m[0], v[0], one)
-    new_w[0] = a.astype(jnp.bfloat16)
-    new_m[0] = b
-    new_v[0] = c
-
-
-def adamw(which, layer, gathered, w, m, v, before):
-    if which < 2:
-        size = 64
-        body, steps = adamw_kernel, D // size
-        g_spec = pl.BlockSpec((size // 16, 2, 16, HALF), lambda i: (i, 0, 0, which))
-        spec = pl.BlockSpec((1, size, FF), lambda i: (layer, i, 0))
-    else:
-        body, steps = adamw_down_kernel, FF // 128
-        g_spec = pl.BlockSpec((64, 1, 16, 128), lambda i: (0, i // 13, 0, 26 + i % 13))
-        spec = pl.BlockSpec((1, 128, D), lambda i: (layer, i, 0))
+ROWS = 64
+STEPS = (D // ROWS, D // ROWS, FF // 128)
+
+
+def adamw_kernel(*refs):
+    g, w, m, v = (refs[i : i + 3] for i in (0, 3, 6, 9))
+    new_w, new_m, new_v = refs[-9:-6], refs[-6:-3], refs[-3:]
+    i = pl.program_id(0)
+    start = 0
+    for n in range(3):
+
+        @pl.when((i >= start) & (i < start + STEPS[n]))
+        def _(n=n):
+            if n < 2:
+                parts = [(slice(half * HALF, (half + 1) * HALF), g[n][:, half].reshape(ROWS, HALF)) for half in range(2)]
+            else:
+                parts = [(slice(None), g[n][:, 0].reshape(D, 128).T)]
+            for columns, one in parts:
+                at = (0, slice(None), columns)
+                a, b, c = update(w[n][at].astype(jnp.float32), m[n][at], v[n][at], one.astype(jnp.float32))
+                new_w[n][at] = a.astype(jnp.bfloat16)
+                new_m[n][at] = b
+                new_v[n][at] = c
+
+        start += STEPS[n]
+
+
+def adamw(layer, gathered, w, m, v, before):
+    def at(n):
+        start = sum(STEPS[:n])
+        return lambda i: jnp.clip(i - start, 0, STEPS[n] - 1)
+
+    def down(i):
+        i = at(2)(i)
+        return 0, i // 13, 0, 26 + i % 13
+
+    g_specs = [pl.BlockSpec((ROWS // 16, 2, 16, HALF), lambda i, n=n: (at(n)(i), 0, 0, n)) for n in range(2)]
+    g_specs.append(pl.BlockSpec((64, 1, 16, 128), down))
+    specs = [pl.BlockSpec((1, ROWS, FF), lambda i, n=n: (layer, at(n)(i), 0)) for n in range(2)]
+    specs.append(pl.BlockSpec((1, 128, D), lambda i: (layer, at(2)(i), 0)))
     more = [] if before is None else list(before)
-    shapes = [jax.ShapeDtypeStruct(w.shape, t) for t in (jnp.bfloat16, jnp.float32, jnp.float32)]
+    shapes = [jax.ShapeDtypeStruct(one.shape, t) for t in (jnp.bfloat16, jnp.float32, jnp.float32) for one in w]
     return pl.pallas_call(
-        body,
-        grid=(steps,),
+        adamw_kernel,
+        grid=(sum(STEPS),),
         out_shape=shapes,
-        in_specs=[g_spec, spec, spec, spec] + [pl.BlockSpec(memory_space=pl.ANY)] * len(more),
-        out_specs=[spec] * 3,
-        input_output_aliases={4 + i: i for i in range(len(more))},
-        compiler_params=pltpu.CompilerParams(vmem_limit_bytes=50_000_000),
-        cost_estimate=pl.CostEstimate(flops=20 * D * FF, bytes_accessed=22 * D * FF, transcendentals=D * FF),
-        name=f"adamw_{which}_{layer}",
-    )(gathered, w, m, v, *more)
+        in_specs=g_specs + specs * 3 + [pl.BlockSpec(memory_space=pl.ANY)] * len(more),
+        out_specs=specs * 3,
+        input_output_aliases={12 + i: i for i in range(len(more))},
+        compiler_params=pltpu.CompilerParams(vmem_limit_bytes=60_000_000),
+        cost_estimate=pl.CostEstimate(flops=60 * D * FF, bytes_accessed=66 * D * FF, transcendentals=3 * D * FF),
+        name=f"adamw_{layer}",
+    )(gathered, gathered, gathered, *w, *m, *v, *more)
 
 
 def by_owner(t, first):
@@ -235,36 +336,26 @@
 def solution(mesh):
     def step(x, dy, *arrays):
         weights, m, v = (arrays[i : i + 3] for i in (0, 3, 6))
-        layers = weights[0].shape[0]
         w_gate, w_up, w_down = weights
-        h, kept = x[0], []
-        for n in range(layers):
-            a, back = jax.vjp(normed, h)
-            gate = jnp.dot(a, w_gate[n], preferred_element_type=jnp.float32)
-            up = jnp.dot(a, w_up[n], preferred_element_type=jnp.float32)
-            hidden = (jax.nn.silu(gate) * up).astype(jnp.bfloat16)
-            kept.append((a, back, gate, up, hidden))
-            if n < layers - 1:
-                h = h + matmul(hidden, w_down[n])
-        by_h, gathered = dy[0], [None] * layers
-        for n in reversed(range(layers)):
-            a, back, gate, up, hidden = kept[n]
-            by_hidden = matmul_t(by_h, w_down[n]).astype(jnp.float32)
-            sig = jax.nn.sigmoid(gate)
-            silu = gate * sig
-            by_up = (by_hidden * silu).astype(jnp.bfloat16)
-            by_gate = (by_hidden * up * (sig + silu * (1 - sig))).astype(jnp.bfloat16)
-            a_t, by_h_t = a.T, by_h.T
-            lhs = [by_owner(a_t, 0), by_owner(a_t, 1), by_owner(by_h_t, 2)]
-            chunk = exchange(lhs, [by_gate, by_up, hidden], n)
-            gathered[n] = lax.all_gather(chunk, "dp", axis=0, tiled=False).reshape(64, 2, 16, 3 * HALF)
-            if n:
-                (by_in,) = back(matmul_t(by_gate, w_gate[n]) + matmul_t(by_up, w_up[n]))
-                by_h = by_h + by_in
-        new = [None] * 3
-        for n in reversed(range(layers)):
-            new = [adamw(i, n, gathered[n], weights[i], m[i], v[i], new[i]) for i in range(3)]
-        return tuple(one[which] for which in range(3) for one in new)
+        states, by_y = x[0], dy[0]
+        a = normed(states)
+        gate, up, hidden, middle, b = over_hidden(forward_kernel, "forward", 0, "ssccr", "fftss", 1, 3, states, a, w_gate, w_up, w_down)
+        last_hidden, by_gate, by_up = over_hidden(last_layer_kernel, "last_layer", 1, "ssccr", "ttt", 0, 3, by_y, b, w_gate, w_up, w_down)
+
+        def sums(number, a, by_h, by_gate, by_up, hidden):
+            a_t = a.T
+            lhs = [by_owner(a_t, 0), by_owner(a_t, 1), by_owner(by_h.T, 2)]
+            chunk = exchange(lhs, [by_gate, by_up, hidden], number)
+            return lax.all_gather(chunk, "dp", axis=0, tiled=False).reshape(64, 2, 16, 3 * HALF)
+
+        gathered = [None, sums(1, b, by_y, by_gate, by_up, last_hidden)]
+        (by_middle,) = over_hidden(by_input_kernel, "by_input", 1, "ssttcc", "s", 2, 2, middle, by_y, by_gate, by_up, w_gate, w_up)
+        by_gate, by_up = over_hidden(backward_kernel, "backward", 0, "srff", "tt", 0, 1, by_middle, w_down, gate, up)
+        gathered[0] = sums(0, a, by_middle, by_gate, by_up, hidden)
+        new = None
+        for n in (1, 0):
+            new = adamw(n, gathered[n], weights, m, v, new)
+        return tuple(new)
 
     return jax.shard_map(
         step,

time: 534 us -> 522 us (0.978)
  matrix products: 127 us -> 0 us
  Pallas kernels: 357 us -> 463 us
  local copies, waits for them, and re-layouts: 13.7 us -> 29.8 us
  other arithmetic: 11.9 us -> 4.26 us
    dot_general x9 -> x0, matrix products: 127 us -> none  [the longest x4 54.5 us: matmul_t(): lax.dot_general(a, w, (((1,), (1,)), ((), ())), preferred_element_type=jn...]
    pallas_call x6, Pallas kernels: 191 us -> 310 us  [the longest x2 184 us: adamw(): pl.pallas_call(adamw_kernel, grid=(sum(STEPS),), out_shape=shapes, in_spe...]
    pallas_call x2, Pallas kernels: 166 us -> 154 us  [exchange(): pl.pallas_call(exchange_kernel, out_shape=jax.ShapeDtypeStruct((16, 3 * H...]
    transpose x0 -> x2, local copies, waits for them, and re-layouts: none -> 8.02 us  [sums(): lhs = [by_owner(a_t, 0), by_owner(a_t, 1), by_owner(by_h.T, 2)]]
  transfers between devices with their start and end apart: 2 -> 2, of which waited for: 0 -> 0; matrix products, arithmetic and copies ran while one was open for 10% -> 2% of each run, Pallas kernels for 35% -> 44%
where the time goes in v2:
time: 522 us; the launch traced here: 512 us
  Pallas kernels  463 us (89%)
  local copies, waits for them, and re-layouts  29.8 us (6%)
  between operations  14.6 us (3%)
    pallas_call x2, Pallas kernels, adamw(): pl.pallas_call(adamw_kernel, grid=(sum(STEPS),), out_shape=shapes, in_spe...  184 us
    pallas_call x2, Pallas kernels, exchange(): pl.pallas_call(exchange_kernel, out_shape=jax.ShapeDtypeStruct((16, 3 * H...  154 us
    pallas_call x4, Pallas kernels, over_hidden(): pl.pallas_call(body, grid=(FF // TILE,), in_specs=[specs[k] for k in kind...  126 us
  transfers between devices with their start and end apart: 2, of which 0 were waited for; matrix products, arithmetic and copies ran while one was open for 2% of the time, Pallas kernels for 44%

profile of v2, /device:TPU:0, one launch (start us, length us, event | category | flops | bytes accessed | tf_op | source)
XLA Modules:
  0.0 512.3 jit_solution(2086362558447495432)
XLA Ops:
  7.2 0.0 all-gather.7.cloned.1.call-start
  7.2 2.9 copy.37
  10.1 0.0 copy-start
  10.1 0.5 fusion
  10.6 0.0 copy-start.3
  10.6 0.8 copy-done.3
  11.4 1.9 fusion.1
  13.3 3.9 copy.40.a
  17.2 3.9 copy.45
  21.1 0.0 copy-done
  21.1 3.2 copy.46
  24.4 35.8 %forward.1 = (f32[1024,3328]{1,0:T(8,128)}, f32[1024,3328]{1,0:T(8,128)}, bf16[1024,3328]{1,0:T(8,128)(2,1)}, bf16[1024,1024]{1,0:T(8,128)(2,1)}, bf16[1024,1024]{1,0:T(8,128)(2,1)}) custom-call(bf16[1024,1024]{1,0:T(8,128)(2,1)} %bitcast.45, bf16[1024,1024]{1,0:T(8,128)(2,1)} %copy.40.a, bf16[2,1024,3328]{2,1,0:T(8,128)(2,1)} %refs_3_.3, ...), custom_call_target="tpu_custom_call" | custom-call | flops 20937965568 | bytes 40000000 | tf_op jit(solution)/shard_map/forward/pallas_call | solution.py:112
  60.2 2.9 copy.43
  63.0 0.0 copy-start.2
  63.1 1.7 copy.44
  64.7 28.9 %last_layer.1 = (bf16[1024,3328]{1,0:T(8,128)(2,1)}, bf16[1024,3328]{1,0:T(8,128)(2,1)}, bf16[1024,3328]{1,0:T(8,128)(2,1)}) custom-call(bf16[1024,1024]{1,0:T(8,128)(2,1)} %bitcast.47, bf16[1024,1024]{1,0:T(8,128)(2,1)} %get-tuple-element.29.a, bf16[2,1024,3328]{2,1,0:T(8,128)(2,1)} %refs_3_.3, bf16[2,1024,3328]{2,1,0:T(8,128)(2,1)} %refs_4_.3, ...), custom_call_target="tpu_custom_call" | custom-call | flops 20937965568 | bytes 40000000 | tf_op jit(solution)/shard_map/last_layer/pallas_call | solution.py:112
  93.7 0.0 copy-done.2
  93.7 80.2 %exchange_1.1 = bf16[16,4992]{1,0:T(8,128)(2,1)} custom-call(bf16[1024,1024]{1,0:T(8,128)(2,1)} %bitcast.41, bf16[1024,1024]{1,0:T(8,128)(2,1)} %bitcast.52, bf16[1024,1024]{1,0:T(8,128)(2,1)} %bitcast.50, bf16[1024,3328]{1,0:T(8,128)(2,1)} %get-tuple-element.30.by_gate.r0, bf16[1024,3328]{1,0:T(8,128)(2,1)} %get-tuple-element.31.by_up.r1, ...), custom_call_target="tpu_custom_call" | custom-call | flops 20937965568 | bytes 26000000 | tf_op jit(solution)/shard_map/exchange_1/pallas_call | solution.py:243
  173.9 0.0 all-gather.7.cloned.1.call-update
  173.9 0.0 all-gather.5.cloned.1.call-start
  173.9 3.2 copy.38
  177.2 35.8 %by_input.1.by_h = bf16[1024,1024]{1,0:T(8,128)(2,1)} custom-call(bf16[1024,1024]{1,0:T(8,128)(2,1)} %get-tuple-element.28.h, bf16[1024,1024]{1,0:T(8,128)(2,1)} %bitcast.48, bf16[1024,3328]{1,0:T(8,128)(2,1)} %get-tuple-element.30.by_gate.r0, bf16[1024,3328]{1,0:T(8,128)(2,1)} %get-tuple-element.31.by_up.r1, bf16[2,1024,3328]{2,1,0:T(8,128)(2,1)} %refs_3_.3, ...), custom_call_target="tpu_custom_call" | custom-call | flops 13958643712 | bytes 40000000 | tf_op jit(solution)/shard_map/by_input/pallas_call | solution.py:112
  212.9 0.0 copy-start.1
  212.9 0.0 copy-start.4
  212.9 4.1 copy.41
  217.0 3.2 copy.42
  220.3 0.0 copy-done.1
  220.3 0.0 copy-done.4
  220.3 1.9 fusion.2.l0
  222.2 25.0 %backward.1 = (bf16[1024,3328]{1,0:T(8,128)(2,1)}, bf16[1024,3328]{1,0:T(8,128)(2,1)}) custom-call(bf16[1024,1024]{1,0:T(8,128)(2,1)} %by_input.1.by_h, bf16[2,3328,1024]{2,1,0:T(8,128)(2,1)} %refs_5_.3, f32[1024,3328]{1,0:T(8,128)} %get-tuple-element.32.gate, f32[1024,3328]{1,0:T(8,128)} %get-tuple-element.33.up), custom_call_target="tpu_custom_call" | custom-call | flops 6979321856 | bytes 40000000 | tf_op jit(solution)/shard_map/backward/pallas_call | solution.py:112
  247.2 73.5 %exchange_0.1 = bf16[16,4992]{1,0:T(8,128)(2,1)} custom-call(bf16[1024,1024]{1,0:T(8,128)(2,1)} %fusion.2.l0, bf16[1024,1024]{1,0:T(8,128)(2,1)} %bitcast.49, bf16[1024,1024]{1,0:T(8,128)(2,1)} %bitcast.51, bf16[1024,3328]{1,0:T(8,128)(2,1)} %get-tuple-element.34.r0, bf16[1024,3328]{1,0:T(8,128)(2,1)} %get-tuple-element.35.r1, ...), custom_call_target="tpu_custom_call" | custom-call | flops 20937965568 | bytes 26000000 | tf_op jit(solution)/shard_map/exchange_0/pallas_call | solution.py:243
  320.7 0.0 all-gather.5.cloned.1.call-update
  320.7 0.0 all-gather.7.cloned.1.call-done
  320.8 92.1 %adamw_1.1 = (bf16[2,1024,3328]{2,1,0:T(8,128)(2,1)}, bf16[2,1024,3328]{2,1,0:T(8,128)(2,1)}, bf16[2,3328,1024]{2,1,0:T(8,128)(2,1)}, f32[2,1024,3328]{2,1,0:T(8...) custom-call(bf16[64,2,16,4992]{3,2,1,0:T(8,128)(2,1)} %bitcast.33, ...), custom_call_target="tpu_custom_call" | custom-call | flops 204472320 | bytes 224919552 | tf_op jit(solution)/shard_map/adamw_1/pallas_call | solution.py:317
  412.9 0.0 all-gather.5.cloned.1.call-done
  412.9 92.1 %adamw_0.1 = (bf16[2,1024,3328]{2,1,0:T(8,128)(2,1)}, bf16[2,1024,3328]{2,1,0:T(8,128)(2,1)}, bf16[2,3328,1024]{2,1,0:T(8,128)(2,1)}, f32[2,1024,3328]{2,1,0:T(8...) custom-call(bf16[64,2,16,4992]{3,2,1,0:T(8,128)(2,1)} %bitcast.36, ...), custom_call_target="tpu_custom_call", output_to_operand_aliasing={{0}: (12, {}), {1}: (13, {}), {2}: (14, {}), {3}: (15, {}),... | custom-call | flops 204472320 | bytes 224919552 | tf_op jit(solution)/shard_map/adamw_0/pallas_call | solution.py:317
  (1 shorter events, 0.0 us)
Async XLA Ops:
  7.2 313.6 %all-gather.7.cloned.1.call-start = ((), (), s32[]{:S(2)}) async-start(), calls=%async_computation.1 | async-start | bytes 20606976 | tf_op jit(solution)/shard_map/all_gather | solution.py:349
  10.1 11.0 %copy-start = (bf16[1,1024,1024]{1,2,0:T(8,128)(2,1)}, bf16[1,1024,1024]{1,2,0:T(8,128)(2,1)S(1)}, u32[]{:S(2)}) copy-start(bf16[1,1024,1024]{1,2,0:T(8,128)(2,1)S(1)} %copy.37) | copy-start | bytes 6291460
  10.6 0.8 copy-start.3
  63.0 30.6 %copy-start.2 = (bf16[1024,1024]{0,1:T(8,128)(2,1)}, bf16[1024,1024]{0,1:T(8,128)(2,1)S(1)}, u32[]{:S(2)}) copy-start(bf16[1024,1024]{0,1:T(8,128)(2,1)S(1)} %copy.43) | copy-start | bytes 6291460
  173.9 239.0 %all-gather.5.cloned.1.call-start = ((), (), s32[]{:S(2)}) async-start(), calls=%async_computation | async-start | bytes 20606976 | tf_op jit(solution)/shard_map/all_gather | solution.py:349
  212.9 7.3 %copy-start.1 = (bf16[1,1024,1024]{1,2,0:T(8,128)(2,1)S(1)}, bf16[1,1024,1024]{1,2,0:T(8,128)(2,1)}, u32[]{:S(2)}) copy-start(bf16[1,1024,1024]{1,2,0:T(8,128)(2,1)} %copy-done) | copy-start | bytes 6291460
  212.9 7.3 %copy-start.4 = (f32[1024]{0:T(1024)S(1)}, f32[1024]{0:T(1024)}, u32[]{:S(2)}) copy-start(f32[1024]{0:T(1024)} %copy-done.3) | copy-start | bytes 12292
Sparse Core Ops, SparseCore 0:
  174.0 82.1 all-gather.6
  320.9 82.6 all-gather.4

commit v3 on v2

--- a/solution.py
+++ b/solution.py
@@ -48,7 +48,11 @@
     return pl.program_id(0) == pl.num_programs(0) - 1
 
 
-def forward_kernel(h, a, w_gate, w_up, w_down, gate, up, hidden, next_h, next_a, total):
+def forward_kernel(h, w_gate, w_up, w_down, gate, up, hidden, a, next_h, next_a, total):
+    @pl.when(pl.program_id(0) == 0)
+    def _():
+        a[...] = normed(h[...])
+
     gate[...] = dot(a[...], w_gate[0])
     up[...] = dot(a[...], w_up[0])
     hidden[...] = (jax.nn.silu(gate[...]) * up[...]).astype(jnp.bfloat16)
@@ -76,21 +80,8 @@
     hidden[...] = (silu * up).astype(jnp.bfloat16)
 
 
-def backward_kernel(by_h, w_down, gate, up, by_gate, by_up):
-    _, by_gate[...], by_up[...] = by_gate_and_up(gate[...], up[...], dot_t(by_h[...], w_down[0]))
-
-
-def by_input_kernel(h, by_h, by_gate, by_up, w_gate, w_up, by_in, total_gate, total_up):
-    add_up(total_gate, dot_t(by_gate[...], w_gate[0]))
-    add_up(total_up, dot_t(by_up[...], w_up[0]))
-
-    @pl.when(last())
-    def _():
-        by_a = (total_gate[...].astype(jnp.bfloat16) + total_up[...].astype(jnp.bfloat16)).astype(jnp.float32)
-        wide = h[...].astype(jnp.float32)
-        scale = scale_of(wide)
-        shared = jnp.sum(by_a * wide, -1, keepdims=True) * scale**3 / D
-        by_in[...] = by_h[...] + (by_a * scale - wide * shared).astype(jnp.bfloat16)
+def matmul_t(a, w):
+    return dot_t(a, w).astype(jnp.bfloat16)
 
 
 TILE = 256
@@ -122,7 +113,7 @@
     )(*args)
 
 
-def exchange_kernel(l0, l1, l2, r0, r1, r2, out, lhs, rhs, mine, part, got_a, got_b, got_c, total, load, core_s, core_r, a_s, a_r, b_s, b_r, c_s, c_r):
+def exchange_kernel(a, by_h, r0, r1, r2, out, lhs, rhs, mine, part, got_a, got_b, got_c, total, load, core_s, core_r, a_s, a_r, b_s, b_r, c_s, c_r):
     me = lax.axis_index("dp")
     core = lax.rem(me, 2)
     partner = me + 1 - 2 * core
@@ -135,11 +126,27 @@
         there = lax.rem(place[axis] + k, SIDE)
         return me + (there - place[axis]) * STRIDE[axis], there
 
-    loads = []
-    for n, (src, dst) in enumerate([(l2, lhs.at[2]), (r2, rhs.at[2]), (l0, lhs.at[0]), (r0, rhs.at[0]), (l1, lhs.at[1]), (r1, rhs.at[1])]):
-        copy = pltpu.make_async_copy(src, dst, load.at[n])
-        copy.start()
-        loads.append(copy)
+    order = (2, 0, 1)
+    states = []
+    for n, (src, dst) in enumerate(((by_h, part), (a, mine))):
+        for quarter in range(4):
+            copy = pltpu.make_async_copy(src.at[pl.ds(256 * quarter, 256)], dst.at[quarter, :, pl.ds(0, D)], load.at[4 * n + quarter])
+            copy.start()
+            states.append(copy)
+    loads = {}
+    for m in order:
+        loads[m] = pltpu.make_async_copy((r0, r1, r2)[m], rhs.at[m], load.at[8 + m])
+        loads[m].start()
+    for n, (held, products) in enumerate(((part, (2,)), (mine, (0, 1)))):
+        for quarter in range(4):
+            states[4 * n + quarter].wait()
+            for block in range(D // 128):
+                turned = held[quarter, :, 128 * block : 128 * (block + 1)].T
+                for i in range(8):
+                    at = (block // 2, 2 * (block % 2) + i // 4, i % 4)
+                    for m in products:
+                        row = 16 * (16 * at[m] + 4 * at[(m + 1) % 3] + at[(m + 2) % 3])
+                        lhs[m, row : row + 16, 256 * quarter : 256 * (quarter + 1)] = turned[16 * i : 16 * (i + 1)]
     barrier = pltpu.get_barrier_semaphore()
     pl.semaphore_signal(barrier, inc=1, **to(partner))
     for axis in range(3):
@@ -150,7 +157,6 @@
     def rows(index, size):
         return pl.ds(pl.multiple_of(index * size, size), size)
 
-    order = (2, 0, 1)
     units = [(m, step) for step in range(4) for m in order]
 
     def block_of(m, step):
@@ -165,8 +171,7 @@
     def give(n):
         m, step = units[n]
         if step == 0:
-            loads[2 * order.index(m)].wait()
-            loads[2 * order.index(m) + 1].wait()
+            loads[m].wait()
         slot = n % SLOTS
         if n >= SLOTS:
             core_copies[n - SLOTS].wait_send()
@@ -235,7 +240,7 @@
         copy.wait_send()
 
 
-def exchange(lhs, rhs, number):
+def exchange(a, by_h, rhs, number):
     def dma(*shape):
         return pltpu.SemaphoreType.DMA(shape)
 
@@ -243,7 +248,7 @@
     return pl.pallas_call(
         exchange_kernel,
         out_shape=jax.ShapeDtypeStruct((16, 3 * HALF), bf16),
-        in_specs=[pl.BlockSpec(memory_space=pl.ANY)] * 6,
+        in_specs=[pl.BlockSpec(memory_space=pl.ANY)] * 5,
         out_specs=pl.BlockSpec(memory_space=pltpu.VMEM),
         scratch_shapes=[
             pltpu.VMEM((3, D, TOKENS), bf16),
@@ -254,7 +259,7 @@
             {"send": pltpu.VMEM((3, 256, HALF), bf16), "got": pltpu.VMEM((3, 3, 64, HALF), bf16)},
             {"send": pltpu.VMEM((3, 64, HALF), bf16), "got": pltpu.VMEM((3, 3, 16, HALF), bf16)},
             pltpu.VMEM((3, 256, HALF), f32),
-            dma(6),
+            dma(11),
             dma(12),
             dma(12),
             *[dma(3, 3)] * 6,
@@ -262,7 +267,7 @@
         compiler_params=pltpu.CompilerParams(collective_id=number, has_side_effects=True, vmem_limit_bytes=67_043_328),
         cost_estimate=pl.CostEstimate(flops=6 * D * TOKENS * FF, bytes_accessed=26_000_000, transcendentals=0),
         name=f"exchange_{number}",
-    )(*lhs, *rhs)
+    )(a, by_h, *rhs)
 
 
 def update(w, m, v, g):
@@ -272,8 +277,8 @@
     return w - 0.02 * step, m, v
 
 
-ROWS = 64
-STEPS = (D // ROWS, D // ROWS, FF // 128)
+ROWS = 128
+STEPS = (D // ROWS, D // ROWS, FF // 256)
 
 
 def adamw_kernel(*refs):
@@ -286,11 +291,10 @@
         @pl.when((i >= start) & (i < start + STEPS[n]))
         def _(n=n):
             if n < 2:
-                parts = [(slice(half * HALF, (half + 1) * HALF), g[n][:, half].reshape(ROWS, HALF)) for half in range(2)]
+                parts = [((0, slice(None), slice(half * HALF, (half + 1) * HALF)), g[n][:, half].reshape(ROWS, HALF)) for half in range(2)]
             else:
-                parts = [(slice(None), g[n][:, 0].reshape(D, 128).T)]
-            for columns, one in parts:
-                at = (0, slice(None), columns)
+                parts = [((0, half, 0), g[n][:, half].reshape(D, 128).T) for half in range(2)]
+            for at, one in parts:
                 a, b, c = update(w[n][at].astype(jnp.float32), m[n][at], v[n][at], one.astype(jnp.float32))
                 new_w[n][at] = a.astype(jnp.bfloat16)
                 new_m[n][at] = b
@@ -305,13 +309,12 @@
         return lambda i: jnp.clip(i - start, 0, STEPS[n] - 1)
 
     def down(i):
-        i = at(2)(i)
-        return 0, i // 13, 0, 26 + i % 13
+        return 0, 0, 0, 26 + at(2)(i)
 
     g_specs = [pl.BlockSpec((ROWS // 16, 2, 16, HALF), lambda i, n=n: (at(n)(i), 0, 0, n)) for n in range(2)]
-    g_specs.append(pl.BlockSpec((64, 1, 16, 128), down))
+    g_specs.append(pl.BlockSpec((64, 2, 16, 128), down))
     specs = [pl.BlockSpec((1, ROWS, FF), lambda i, n=n: (layer, at(n)(i), 0)) for n in range(2)]
-    specs.append(pl.BlockSpec((1, 128, D), lambda i: (layer, at(2)(i), 0)))
+    specs.append(pl.BlockSpec((1, 2, 1, 128, D), lambda i: (layer, 0, at(2)(i), 0, 0)))
     more = [] if before is None else list(before)
     shapes = [jax.ShapeDtypeStruct(one.shape, t) for t in (jnp.bfloat16, jnp.float32, jnp.float32) for one in w]
     return pl.pallas_call(
@@ -321,16 +324,10 @@
         in_specs=g_specs + specs * 3 + [pl.BlockSpec(memory_space=pl.ANY)] * len(more),
         out_specs=specs * 3,
         input_output_aliases={12 + i: i for i in range(len(more))},
-        compiler_params=pltpu.CompilerParams(vmem_limit_bytes=60_000_000),
+        compiler_params=pltpu.CompilerParams(vmem_limit_bytes=64_000_000),
         cost_estimate=pl.CostEstimate(flops=60 * D * FF, bytes_accessed=66 * D * FF, transcendentals=3 * D * FF),
         name=f"adamw_{layer}",
     )(gathered, gathered, gathered, *w, *m, *v, *more)
-
-
-def by_owner(t, first):
-    blocks = t.reshape(SIDE, SIDE, SIDE, 16, t.shape[1])
-    order = [(first + i) % 3 for i in range(3)]
-    return blocks.transpose(*order, 3, 4).reshape(t.shape)
 
 
 def solution(mesh):
@@ -338,24 +335,23 @@
         weights, m, v = (arrays[i : i + 3] for i in (0, 3, 6))
         w_gate, w_up, w_down = weights
         states, by_y = x[0], dy[0]
-        a = normed(states)
-        gate, up, hidden, middle, b = over_hidden(forward_kernel, "forward", 0, "ssccr", "fftss", 1, 3, states, a, w_gate, w_up, w_down)
+        gate, up, hidden, a, middle, b = over_hidden(forward_kernel, "forward", 0, "sccr", "fftsss", 1, 3, states, w_gate, w_up, w_down)
         last_hidden, by_gate, by_up = over_hidden(last_layer_kernel, "last_layer", 1, "ssccr", "ttt", 0, 3, by_y, b, w_gate, w_up, w_down)
 
-        def sums(number, a, by_h, by_gate, by_up, hidden):
-            a_t = a.T
-            lhs = [by_owner(a_t, 0), by_owner(a_t, 1), by_owner(by_h.T, 2)]
-            chunk = exchange(lhs, [by_gate, by_up, hidden], number)
+        def sums(number, a, by_h, *rhs):
+            chunk = exchange(a, by_h, rhs, number)
             return lax.all_gather(chunk, "dp", axis=0, tiled=False).reshape(64, 2, 16, 3 * HALF)
 
         gathered = [None, sums(1, b, by_y, by_gate, by_up, last_hidden)]
-        (by_middle,) = over_hidden(by_input_kernel, "by_input", 1, "ssttcc", "s", 2, 2, middle, by_y, by_gate, by_up, w_gate, w_up)
-        by_gate, by_up = over_hidden(backward_kernel, "backward", 0, "srff", "tt", 0, 1, by_middle, w_down, gate, up)
+        _, back = jax.vjp(normed, middle)
+        by_middle = by_y + back(matmul_t(by_gate, w_gate[1]) + matmul_t(by_up, w_up[1]))[0]
+        _, by_gate, by_up = by_gate_and_up(gate, up, dot_t(by_middle, w_down[0]))
         gathered[0] = sums(0, a, by_middle, by_gate, by_up, hidden)
         new = None
+        split = [(*one[:2], one[2].reshape(2, 2, FF // 256, 128, D)) for one in (weights, m, v)]
         for n in (1, 0):
-            new = adamw(n, gathered[n], weights, m, v, new)
-        return tuple(new)
+            new = adamw(n, gathered[n], *split, new)
+        return tuple(one.reshape(2, *one.shape[-2:]) if one.ndim == 3 else one.reshape(2, FF, D) for one in new)
 
     return jax.shard_map(
         step,

time: 522 us -> 468 us (0.90)
  Pallas kernels: 463 us -> 399 us
  matrix products: 0 us -> 46.1 us
  local copies, waits for them, and re-layouts: 29.8 us -> 0.02 us
    pallas_call x4 -> x2, Pallas kernels: 126 us -> 65.6 us  [over_hidden(): pl.pallas_call(body, grid=(FF // TILE,), in_specs=[specs[k] for k in kind...]
    dot_general x0 -> x3, matrix products: none -> 46.1 us  [dot_t(): lax.dot_general(a, w, (((1,), (1,)), ((), ())), preferred_element_type=jn...]
    pallas_call x2, Pallas kernels: 184 us -> 164 us  [adamw(): pl.pallas_call(adamw_kernel, grid=(sum(STEPS),), out_shape=shapes, in_spe...]
    pallas_call x2, Pallas kernels: 154 us -> 169 us  [exchange(): pl.pallas_call(exchange_kernel, out_shape=jax.ShapeDtypeStruct((16, 3 * H...]
    transpose x4 -> x0, local copies, waits for them, and re-layouts: 14.5 us -> none  [the longest x2 8.02 us: sums(): lhs = [by_owner(a_t, 0), by_owner(a_t, 1), by_owner(by_h.T, 2)]]
  transfers between devices with their start and end apart: 2 -> 2, of which waited for: 0 -> 1; matrix products, arithmetic and copies ran while one was open for 2% -> 10% of each run, Pallas kernels for 44% -> 37%
where the time goes in v3:
time: 468 us; the launch traced here: 461 us
  Pallas kernels  399 us (85%)
  matrix products  46.1 us (10%)
  between operations  14.6 us (3%)
    pallas_call x2, Pallas kernels, exchange(): pl.pallas_call(exchange_kernel, out_shape=jax.ShapeDtypeStruct((16, 3 * H...  169 us
    pallas_call x2, Pallas kernels, adamw(): pl.pallas_call(adamw_kernel, grid=(sum(STEPS),), out_shape=shapes, in_spe...  164 us
    pallas_call x2, Pallas kernels, over_hidden(): pl.pallas_call(body, grid=(FF // TILE,), in_specs=[specs[k] for k in kind...  65.6 us
    dot_general x3, matrix products, dot_t(): lax.dot_general(a, w, (((1,), (1,)), ((), ())), preferred_element_type=jn...  46.1 us
  transfers between devices with their start and end apart: 2, of which 1 were waited for; matrix products, arithmetic and copies ran while one was open for 10% of the time, Pallas kernels for 37%

profile of v3, /device:TPU:0, one launch (start us, length us, event | category | flops | bytes accessed | tf_op | source)
XLA Modules:
  0.0 461.3 jit_solution(16892785276688917363)
XLA Ops:
  7.2 0.0 all-gather.7.cloned.1.call-start
  7.2 36.6 %forward.1 = (f32[1024,3328]{1,0:T(8,128)}, f32[1024,3328]{1,0:T(8,128)}, bf16[1024,3328]{1,0:T(8,128)(2,1)}, bf16[1024,1024]{1,0:T(8,128)(2,1)}, bf16[1024,1024...) custom-call(bf16[1024,1024]{1,0:T(8,128)(2,1)} %bitcast.46, bf16[2,1024,3328]{2,1,0:T(8,128)(2,1)} %refs_3_.3, ...), custom_call_target="tpu_custom_call" | custom-call | flops 20937965568 | bytes 40000000 | tf_op jit(solution)/shard_map/forward/pallas_call | solution.py:103
  43.8 29.0 %last_layer.1 = (bf16[1024,3328]{1,0:T(8,128)(2,1)}, bf16[1024,3328]{1,0:T(8,128)(2,1)}, bf16[1024,3328]{1,0:T(8,128)(2,1)}) custom-call(bf16[1024,1024]{1,0:T(8,128)(2,1)} %bitcast.44, bf16[1024,1024]{1,0:T(8,128)(2,1)} %get-tuple-element.37.a, bf16[2,1024,3328]{2,1,0:T(8,128)(2,1)} %refs_3_.3, bf16[2,1024,3328]{2,1,0:T(8,128)(2,1)} %refs_4_.3, ...), custom_call_target="tpu_custom_call" | custom-call | flops 20937965568 | bytes 40000000 | tf_op jit(solution)/shard_map/last_layer/pallas_call | solution.py:103
  72.8 79.7 %exchange_1.1 = bf16[16,4992]{1,0:T(8,128)(2,1)} custom-call(bf16[1024,1024]{1,0:T(8,128)(2,1)} %get-tuple-element.37.a, bf16[1024,1024]{1,0:T(8,128)(2,1)} %bitcast.45, bf16[1024,3328]{1,0:T(8,128)(2,1)} %get-tuple-element.38.r0, bf16[1024,3328]{1,0:T(8,128)(2,1)} %get-tuple-element.39.r1, bf16[1024,3328]{1,0:T(8,128)(2,1)} %get-tuple-element.44.r2), custom_call_target="tpu_custom_call" | custom-call | flops 20937965568 | bytes 26000000 | tf_op jit(solution)/shard_map/exchange_1/pallas_call | solution.py:248
  152.5 0.0 all-gather.7.cloned.1.call-update
  152.5 0.0 copy-start.1
  152.6 0.0 all-gather.5.cloned.1.call-start
  152.6 11.6 %fusion.5 = bf16[1024,1024]{1,0:T(8,128)(2,1)S(1)} fusion(bf16[1024,3328]{1,0:T(8,128)(2,1)} %get-tuple-element.39.r1, bf16[2,1024,3328]{2,1,0:T(8,128)(2,1)} %refs_4_.3), kind=kOutput, calls=%fused_computation.9 | convolution fusion | flops 6979321856 | bytes 15728640 | tf_op jit(solution)/shard_map/dot_general | solution.py:32
  164.2 0.0 copy-done.1
  164.2 0.0 copy-start
  164.2 11.9 %fusion.14 = (f32[1024]{0:T(1024)S(1)}, f32[1024]{0:T(1024)S(1)}, bf16[1024,1024]{1,0:T(8,128)(2,1)S(1)}) fusion(bf16[1024,1024]{1,0:T(8,128)(2,1)S(1)} %copy-done.1, bf16[1024,1024]{1,0:T(8,128)(2,1)S(1)} %fusion.5, bf16[1024,3328]{1,0:T(8,128)(2,1)} %get-tuple-element.38.r0, bf16[2,1024,3328]{2,1,0:T(8,128)(2,1)} %refs_3_.3), kind=kOutput, calls=%fused_computation.22 | convolution fusion | flops 6987708416 | bytes 19931136 | tf_op jit(solution)/shard_map/dot_general | solution.py:32
  176.1 0.0 copy-done
  176.1 1.1 fusion.16.by_h
  177.2 0.0 copy-start.2
  177.2 22.6 %fusion.2 = (bf16[1024,3328]{1,0:T(8,128)(2,1)}, bf16[1024,3328]{1,0:T(8,128)(2,1)}) fusion(f32[1024,3328]{1,0:T(8,128)} %get-tuple-element.42, f32[1024,3328]{1,0:T(8,128)} %get-tuple-element.41, bf16[1024,1024]{1,0:T(8,128)(2,1)S(1)} %fusion.16.by_h, bf16[2,3328,1024]{2,1,0:T(8,128)(2,1)} %w_down.3), kind=kOutput, calls=%fused_computation.4 | convolution fusion | flops 7027032064 | bytes 49807360 | tf_op jit(solution)/shard_map/dot_general | solution.py:32
  199.9 0.0 copy-done.2
  199.9 89.1 %exchange_0.1 = bf16[16,4992]{1,0:T(8,128)(2,1)} custom-call(bf16[1024,1024]{1,0:T(8,128)(2,1)} %get-tuple-element.36.a, bf16[1024,1024]{1,0:T(8,128)(2,1)} %copy-done.2, bf16[1024,3328]{1,0:T(8,128)(2,1)} %get-tuple-element.66.r0, bf16[1024,3328]{1,0:T(8,128)(2,1)} %get-tuple-element.65.r1, bf16[1024,3328]{1,0:T(8,128)(2,1)} %get-tuple-element.43.r2), custom_call_target="tpu_custom_call" | custom-call | flops 20937965568 | bytes 26000000 | tf_op jit(solution)/shard_map/exchange_0/pallas_call | solution.py:248
  289.0 0.0 all-gather.5.cloned.1.call-update
  289.0 0.0 all-gather.7.cloned.1.call-done
  289.1 82.2 %adamw_1.1 = (bf16[2,1024,3328]{2,1,0:T(8,128)(2,1)}, bf16[2,1024,3328]{2,1,0:T(8,128)(2,1)}, bf16[2,2,13,128,1024]{4,3,2,1,0:T(8,128)(2,1)}, f32[2,1024,3328]{2...) custom-call(bf16[64,2,16,4992]{3,2,1,0:T(8,128)(2,1)} %bitcast.29, ...), custom_call_target="tpu_custom_call" | custom-call | flops 204472320 | bytes 224919552 | tf_op jit(solution)/shard_map/adamw_1/pallas_call | solution.py:320
  371.3 0.6 all-gather.5.cloned.1.call-done
  371.9 82.1 %adamw_0.1 = (bf16[2,1024,3328]{2,1,0:T(8,128)(2,1)}, bf16[2,1024,3328]{2,1,0:T(8,128)(2,1)}, bf16[2,2,13,128,1024]{4,3,2,1,0:T(8,128)(2,1)}, f32[2,1024,3328]{2...) custom-call(bf16[64,2,16,4992]{3,2,1,0:T(8,128)(2,1)} %bitcast.32, ...), custom_call_target="tpu_custom_call", output_to_operand_aliasing={{0}: (12, {}), {1}: (13, {}), {2}: (14, {}), {3}: (15, {}),... | custom-call | flops 204472320 | bytes 224919552 | tf_op jit(solution)/shard_map/adamw_0/pallas_call | solution.py:320
  (1 shorter events, 0.0 us)
Async XLA Ops:
  7.2 281.9 %all-gather.7.cloned.1.call-start = ((), (), s32[]{:S(2)}) async-start(), calls=%async_computation.1 | async-start | bytes 20606976 | tf_op jit(solution)/shard_map/all_gather | solution.py:343
  152.5 11.6 %copy-start.1 = (bf16[1024,1024]{1,0:T(8,128)(2,1)S(1)}, bf16[1024,1024]{1,0:T(8,128)(2,1)}, u32[]{:S(2)}) copy-start(bf16[1024,1024]{1,0:T(8,128)(2,1)} %get-tuple-element.40) | copy-start | bytes 6291460
  152.6 219.3 %all-gather.5.cloned.1.call-start = ((), (), s32[]{:S(2)}) async-start(), calls=%async_computation | async-start | bytes 20606976 | tf_op jit(solution)/shard_map/all_gather | solution.py:343
  164.2 12.0 %copy-start = (bf16[1,1024,1024]{2,1,0:T(8,128)(2,1)S(1)}, bf16[1,1024,1024]{2,1,0:T(8,128)(2,1)}, u32[]{:S(2)}) copy-start(bf16[1,1024,1024]{2,1,0:T(8,128)(2,1)} %param.12) | copy-start | bytes 6291460
  177.2 22.7 %copy-start.2 = (bf16[1024,1024]{1,0:T(8,128)(2,1)}, bf16[1024,1024]{1,0:T(8,128)(2,1)S(1)}, u32[]{:S(2)}) copy-start(bf16[1024,1024]{1,0:T(8,128)(2,1)S(1)} %fusion.16.by_h) | copy-start | bytes 6291460
Sparse Core Ops, SparseCore 0:
  152.7 115.6 all-gather.6
  289.2 82.6 all-gather.4
